TPU v7x, 32 devices: a whole 2x2x4 slice. The times are simulated.
32 devices in a mesh: len: 2 (over x), tile: 16 (over z, y, core).
Axes of the slice: x: 2, y: 2, z: 4, core: 2. Of those that a mesh axis runs over, the one named last changes fastest.
Arguments:
- series: float32 [9216], P('tile'), may hold values from -24 to 24
- window_lengths: int32 [4], P('len'), may hold values from 64 to 1024, as said below
- exclusion: int32 [4], P('len'), may hold values from 16 to 256
- tile_list: int32 [64, 2], P('tile'), may hold values from 0 to 15, as said below
Outputs:
- right_profile: float32 [4, 8192], P(None, 'tile')
- left_profile: float32 [4, 8192], P(None, 'tile')
Inputs may be any that keep to these rules, and one draw needn't show every extreme that they name: `window_lengths`: the largest is exactly 1024. `tile_list`: each row is a pair (row block, column block) with row block <= column block; no pair appears twice.
All inputs are finite; a program needn't handle non-finite values.
Results may differ from a plain program's by a relative error of at most 0.00039.
Values sent between devices are 32-bit elements; how exact they have to be, the bound alone decides.
A program may use at most 64 MiB of HBM per device.

v0:
```python
import functools

import jax
import jax.numpy as jnp
from jax import lax
from jax.experimental import pallas as pl
from jax.experimental.pallas import tpu as pltpu
from jax.sharding import PartitionSpec as P

MAX_LEN = 1024
TILE_SIDE = 512
LANES = 128
SUBLANES = 8
GRANT = 1 << 20
QUARTERS = TILE_SIDE // LANES

VAR_EPS = 1e-05

VMEM = pltpu.MemorySpace.VMEM
SMEM = pltpu.MemorySpace.SMEM
HBM = pltpu.MemorySpace.HBM


def partner(me, step, n):
    if n & (n - 1):
        return lax.rem(me + step, n)
    peer = me
    for b in range(n.bit_length() - 1):
        if step >> b & 1:
            peer = peer + (1 << b) * (1 - 2 * lax.rem(lax.div(me, 1 << b), 2))
    return peer


def steps_of(n):
    return range(n - 1, 0, -1)


def signal_all(barrier, axis, n):
    me = lax.axis_index(axis)
    for step in range(1, n) if n & (n - 1) else steps_of(n):
        pl.semaphore_signal(
            barrier,
            inc=1,
            device_id={axis: partner(me, step, n)},
            device_id_type=pl.DeviceIdType.MESH,
        )


def copy_to(axis, n, step, source, target, send_sem, recv_sem):
    return pltpu.make_async_remote_copy(
        src_ref=source,
        dst_ref=target,
        send_sem=send_sem,
        recv_sem=recv_sem,
        device_id={axis: partner(lax.axis_index(axis), step, n)},
        device_id_type=pl.DeviceIdType.MESH,
    )


def shifted(values, count):
    rows = values.shape[0]
    skip, shift = count // LANES, count % LANES
    if shift:
        lane_ids = lax.broadcasted_iota(jnp.int32, values.shape, 1)
        values = pltpu.roll(values, LANES - shift, 1)
        values = jnp.where(lane_ids < LANES - shift, values, pltpu.roll(values, rows - 1, 0))
    if skip:
        values = pltpu.roll(values, rows - skip, 0)
    return values


def window_stats(packed, lengths):
    mean, spread = packed, jnp.zeros_like(packed)
    results = [(jnp.zeros_like(packed), jnp.zeros_like(packed)) for _ in lengths]
    bits = MAX_LEN.bit_length()
    for b in range(bits):
        first = 1 << b
        for l, length in enumerate(lengths):
            tail_mean, tail_spread = results[l]
            if b:
                tail_mean, tail_spread = shifted(tail_mean, first), shifted(tail_spread, first)
            rest = lax.rem(length, first).astype(jnp.float32)
            share = rest / (rest + first)
            gap = tail_mean - mean
            taken = (jnp.full(packed.shape, length) & first) != 0
            results[l] = (
                jnp.where(taken, mean + gap * share, results[l][0]),
                jnp.where(
                    taken, spread + tail_spread + gap * gap * (share * first), results[l][1]
                ),
            )
        if b < bits - 1:
            next_mean = shifted(mean, first)
            gap = next_mean - mean
            mean = 0.5 * (mean + next_mean)
            if b:
                spread = spread + shifted(spread, first) + gap * gap * (0.5 * first)
            else:
                spread = gap * gap * 0.5
    return [
        (mean, 1.0 / jnp.sqrt(spread / length.astype(jnp.float32) + VAR_EPS))
        for (mean, spread), length in zip(results, lengths)
    ]


def profile_kernel(
    piece,
    n,
    count_len,
    len_devices,
    slots_of_tiles,
    series_ref,
    tile_hbm,
    length_hbm,
    barrier_hbm,
    groups,
    piece_ref,
    tile_ref,
    length_ref,
    barrier_ref,
    flat,
    staged,
    slots,
    packed,
    base,
    centre_ref,
    inverse_ref,
    keep_ref,
    left_op,
    right_op,
    best,
    parts,
    mine,
    in_sem,
    send_piece,
    recv_piece,
    send_sem,
    recv_sem,
    send_len,
    recv_len,
):
    me = lax.axis_index("tile")
    my_len = lax.axis_index("len")
    loads = [
        pltpu.make_async_copy(source, target, in_sem.at[k])
        for k, (source, target) in enumerate(
            (
                (series_ref, piece_ref),
                (tile_hbm, tile_ref),
                (length_hbm, length_ref),
                (barrier_hbm, barrier_ref),
            )
        )
    ]
    loads[0].start()
    barrier = pltpu.get_barrier_semaphore()
    signal_all(barrier, "tile", n)
    signal_all(barrier, "len", len_devices)
    for load in loads[1:]:
        load.start()

    slot_rows = staged.shape[0]
    flat[...] = jnp.zeros(flat.shape, jnp.float32)
    loads[0].wait()
    flat[:piece] = piece_ref[...]
    values = flat[...].reshape(slot_rows, LANES)
    shift = lax.rem(me * piece, LANES)
    lane_ids = lax.broadcasted_iota(jnp.int32, values.shape, 1)
    values = pltpu.roll(values, shift, 1)
    staged[...] = jnp.where(lane_ids >= shift, values, pltpu.roll(values, 1, 0))

    pl.semaphore_wait(barrier, n - 1 + len_devices - 1)
    copies = [
        copy_to("tile", n, step, staged, slots.at[me], send_piece.at[step], recv_piece.at[step])
        for step in steps_of(n)
    ]
    for copy in copies:
        copy.start()
    slots[me] = staged[...]
    for load in loads[1:]:
        load.wait()

    lengths = [length_ref[l] for l in range(count_len)]
    row_ids = lax.broadcasted_iota(jnp.int32, (MAX_LEN, LANES), 0)
    row_ids = row_ids + (SUBLANES - 1) - 2 * lax.rem(row_ids, SUBLANES)
    for l, length in enumerate(lengths):
        keep_ref[l] = jnp.where(row_ids < length, 1.0, 0.0).astype(jnp.bfloat16)
        best[l] = jnp.full(best.shape[1:], -length.astype(jnp.float32), jnp.float32)
    packed[...] = jnp.zeros(packed.shape, jnp.float32)
    for copy in copies:
        copy.wait_recv()

    columns = packed.shape[0]
    for t in range(n):
        low, first = divmod(t * piece, LANES)
        used = (first + piece + LANES - 1) // LANES
        packed[low : low + used, :] += slots[t, :used, :]

    for l, (centre, inverse) in enumerate(window_stats(packed[...], lengths)):
        centre_ref[l] = centre.reshape(columns, 1, LANES)
        inverse_ref[l] = inverse.reshape(columns, 1, LANES)

    sub = lax.broadcasted_iota(jnp.int32, (SUBLANES, LANES), 0)
    lane = lax.broadcasted_iota(jnp.int32, (SUBLANES, LANES), 1)
    groups8 = LANES // SUBLANES
    span = 12 if columns % 12 == 0 else 1

    def spread_columns(k, turned):
        for j in range(span):
            a = columns - 1 - k * span - j
            row = jnp.broadcast_to(packed[pl.ds(a, 1), :], (SUBLANES, LANES))
            later = []
            for g in range(groups8):
                moved = pltpu.roll(row, LANES + 1 - SUBLANES * (g + 1), 1, stride=1, stride_axis=0)
                base[a, SUBLANES * g : SUBLANES * (g + 1), :] = jnp.where(
                    lane - sub < LANES + 1 - SUBLANES * (g + 1), moved, turned[g]
                )
                later.append(moved)
            turned = tuple(later)
        return turned

    lax.fori_loop(
        0,
        columns // span,
        spread_columns,
        (jnp.zeros((SUBLANES, LANES), jnp.float32),) * groups8,
    )

    def build(l, slot, buffer):
        firsts = [tile_ref[k, slot] * QUARTERS for k in range(2)]
        for k, (first, target) in enumerate(zip(firsts, (left_op, right_op))):
            for u in range(QUARTERS):
                centre, inverse = centre_ref[l, first + u], inverse_ref[l, first + u]
                for c in range(MAX_LEN // LANES):
                    rows = slice(c * LANES, (c + 1) * LANES)
                    normal = ((base[first + u + c] - centre) * inverse).astype(jnp.bfloat16)
                    if k == 0:
                        normal = normal * keep_ref[l, rows, :]
                    target[buffer, rows, u * LANES : (u + 1) * LANES] = normal

    def product(l, slot, buffer):
        row_block, col_block = tile_ref[0, slot], tile_ref[1, slot]
        size = lengths[l].astype(jnp.float32)
        limit = barrier_ref[l] - (col_block - row_block) * TILE_SIDE
        tops = [None] * QUARTERS
        found = []
        for low in range(0, TILE_SIDE, 2 * LANES):
            values = lax.dot_general(
                left_op[buffer, :, low : low + 2 * LANES],
                right_op[buffer],
                (((0,), (0,)), ((), ())),
                preferred_element_type=jnp.float32,
            )
            ahead = lax.broadcasted_iota(jnp.int32, values.shape, 1) - (
                lax.broadcasted_iota(jnp.int32, values.shape, 0) + low
            )
            values = jnp.where(ahead > limit, values, -size)
            folded = None
            for u in range(QUARTERS):
                part = values[:, u * LANES : (u + 1) * LANES]
                folded = part if folded is None else jnp.maximum(folded, part)
                top = jnp.max(part, axis=0, keepdims=True)
                tops[u] = top if tops[u] is None else jnp.maximum(tops[u], top)
            for q in range(2):
                turned_back = jnp.transpose(folded[q * LANES : (q + 1) * LANES, :])
                found.append(jnp.max(turned_back, axis=0, keepdims=True))
        both = jnp.full((SUBLANES, LANES), -size, jnp.float32)
        for u in range(QUARTERS):
            both = jnp.where(sub == u, found[u], both)
            both = jnp.where(sub == QUARTERS + u, tops[u], both)
        row_is, col_is = jnp.full(sub.shape, row_block), jnp.full(sub.shape, col_block)
        owner = jnp.where(sub < QUARTERS, row_is, col_is)
        for b in range(n):
            old = best[l, b]
            best[l, b] = jnp.where(owner == b, jnp.maximum(old, both), old)

    sends = []
    work = [(l, slot) for l in range(count_len) for slot in range(slots_of_tiles)]
    build(*work[0], 0)
    for p, (l, slot) in enumerate(work):
        if p + 1 < len(work):
            build(*work[p + 1], (p + 1) % 2)
        product(l, slot, p % 2)
        if slot == slots_of_tiles - 1:
            sends.append(
                [
                    copy_to(
                        "tile",
                        n,
                        step,
                        best.at[l, partner(me, step, n)],
                        parts.at[l, step],
                        send_sem.at[l, step],
                        recv_sem.at[l, step],
                    )
                    for step in steps_of(n)
                ]
            )
            for copy in sends[-1]:
                copy.start()

    for l in range(count_len):
        for copy in sends[l]:
            copy.wait_recv()
        merged = best[l, me]
        for step in range(1, n):
            merged = jnp.maximum(merged, parts[l, step])
        merged = 1.0 - merged / lengths[l].astype(jnp.float32)
        mine[l] = merged
        groups[my_len, l] = merged
    copies_len = [
        copy_to("len", len_devices, step, mine, groups.at[my_len], send_len.at[step], recv_len.at[step])
        for step in range(1, len_devices)
    ]
    for copy in copies_len:
        copy.start()
    for copy in copies:
        copy.wait_send()
    for some in sends:
        for copy in some:
            copy.wait_send()
    for copy in copies_len:
        copy.wait()


def write_kernel(groups_ref, right_ref, left_ref, right, left, sems):
    len_devices, count_len = groups_ref.shape[:2]
    for g in range(len_devices):
        for l in range(count_len):
            row = g * count_len + l
            for u in range(QUARTERS):
                lanes = slice(u * LANES, (u + 1) * LANES)
                right[row : row + 1, lanes] = groups_ref[g, l, u : u + 1, :]
                left[row : row + 1, lanes] = groups_ref[g, l, QUARTERS + u : QUARTERS + u + 1, :]
    copies = [
        pltpu.make_async_copy(right, right_ref, sems.at[0]),
        pltpu.make_async_copy(left, left_ref, sems.at[1]),
    ]
    for copy in copies:
        copy.start()
    for copy in copies:
        copy.wait()


def shards(series, window_lengths, exclusion, tile_list):
    n = lax.axis_size("tile")
    len_devices = lax.axis_size("len")
    count_len = window_lengths.shape[0]
    piece = series.shape[0]
    points = piece * n
    columns = points // LANES
    blocks = (points - MAX_LEN) // TILE_SIDE
    assert blocks == n
    slot_rows = (piece + 2 * LANES - 2) // LANES
    slot_rows = (slot_rows + SUBLANES - 1) // SUBLANES * SUBLANES
    depth = (count_len, columns, 1, LANES)
    minima = (count_len, n, SUBLANES, LANES)
    dma = pltpu.SemaphoreType.DMA

    groups = pl.pallas_call(
        functools.partial(
            profile_kernel, piece, n, count_len, len_devices, tile_list.shape[0]
        ),
        out_shape=jax.ShapeDtypeStruct((len_devices, count_len, SUBLANES, LANES), jnp.float32),
        in_specs=[pl.BlockSpec(memory_space=HBM)] * 4,
        out_specs=pl.BlockSpec(memory_space=VMEM),
        scratch_shapes=[
            pltpu.VMEM((piece,), jnp.float32),
            pltpu.SMEM(tile_list.shape[::-1], jnp.int32),
            pltpu.SMEM(window_lengths.shape, jnp.int32),
            pltpu.SMEM(exclusion.shape, jnp.int32),
            pltpu.VMEM((slot_rows * LANES,), jnp.float32),
            pltpu.VMEM((slot_rows, LANES), jnp.float32),
            pltpu.VMEM((n, slot_rows, LANES), jnp.float32),
            pltpu.VMEM((columns, LANES), jnp.float32),
            pltpu.VMEM((columns, LANES, LANES), jnp.float32),
            pltpu.VMEM(depth, jnp.float32),
            pltpu.VMEM(depth, jnp.float32),
            pltpu.VMEM((count_len, MAX_LEN, LANES), jnp.bfloat16),
            pltpu.VMEM((2, MAX_LEN, TILE_SIDE), jnp.bfloat16),
            pltpu.VMEM((2, MAX_LEN, TILE_SIDE), jnp.bfloat16),
            pltpu.VMEM(minima, jnp.float32),
            pltpu.VMEM(minima, jnp.float32),
            pltpu.VMEM((count_len, SUBLANES, LANES), jnp.float32),
            dma((4,)),
            dma((n,)),
            dma((n,)),
            dma((count_len, n)),
            dma((count_len, n)),
            dma((len_devices,)),
            dma((len_devices,)),
        ],
        compiler_params=pltpu.CompilerParams(
            collective_id=0,
            has_side_effects=True,
            vmem_limit_bytes=16 * GRANT + points * LANES * 4,
        ),
        name="profile",
    )(series, tile_list.T, window_lengths, exclusion)

    profile = jax.ShapeDtypeStruct((len_devices * count_len, TILE_SIDE), jnp.float32)
    return pl.pallas_call(
        write_kernel,
        out_shape=(profile, profile),
        in_specs=[pl.BlockSpec(memory_space=VMEM)],
        out_specs=(pl.BlockSpec(memory_space=HBM), pl.BlockSpec(memory_space=HBM)),
        scratch_shapes=[
            pltpu.VMEM(profile.shape, jnp.float32),
            pltpu.VMEM(profile.shape, jnp.float32),
            dma((2,)),
        ],
        name="write_profiles",
    )(groups)


def solution(mesh):
    return jax.shard_map(
        shards,
        mesh=mesh,
        in_specs=(P("tile"), P("len"), P("len"), P("tile", None)),
        out_specs=(P(None, "tile"), P(None, "tile")),
        check_vma=False,
    )
```

profile of v0, /device:TPU:0, one launch (start us, length us, event | category | flops | bytes accessed | tf_op | source)
XLA Modules:
  0.0 35.0 jit_solution(17239783120007035918)
XLA Ops:
  0.6 0.0 copy-start.2
  0.6 0.0 copy-start.3
  0.7 0.7 %copy-done.2 = s32[4,2]{0,1:T(2,128)S(1)} copy-done((s32[4,2]{0,1:T(2,128)S(1)}, s32[4,2]{0,1:T(2,128)}, u32[]{:S(2)}) %copy-start.2) | copy-done | bytes 56
  1.3 0.0 copy-done.3
  1.3 0.0 copy-start.1
  1.3 0.7 %copy-done.1 = f32[576]{0:T(1024)S(1)} copy-done((f32[576]{0:T(1024)S(1)}, f32[576]{0:T(1024)}, u32[]{:S(2)}) %copy-start.1) | copy-done | bytes 2328
  2.0 0.0 copy-start.4
  2.0 0.7 %copy-done.4 = s32[2]{0:T(128)S(1)} copy-done((s32[2]{0:T(128)S(1)}, s32[2]{0:T(128)}, u32[]{:S(2)}) %copy-start.4) | copy-done | bytes 32
  2.7 30.4 %profile.1.groups_ref = f32[2,2,8,128]{3,2,1,0:T(8,128)S(1)} custom-call(f32[576]{0:T(1024)S(1)} %copy-done.1, s32[2,4]{1,0:T(2,128)S(1)} %bitcast.1, s32[2]{0:T(128)S(1)} %copy-done.3, s32[2]{0:T(128)S(1)} %copy-done.4), custom_call_target="tpu_custom_call" | custom-call | tf_op jit(solution)/shard_map/profile/pallas_call | solution.py:360
  33.1 0.0 copy-start
  33.1 0.6 %copy-done = f32[2,2,8,128]{3,2,1,0:T(8,128)} copy-done((f32[2,2,8,128]{3,2,1,0:T(8,128)}, f32[2,2,8,128]{3,2,1,0:T(8,128)S(1)}, u32[]{:S(2)}) %copy-start) | copy-done | bytes 16408
  33.7 1.3 %write_profiles.1 = (f32[4,512]{1,0:T(4,128)}, f32[4,512]{1,0:T(4,128)}) custom-call(f32[2,2,8,128]{3,2,1,0:T(8,128)} %copy-done), custom_call_target="tpu_custom_call" | custom-call | tf_op jit(solution)/shard_map/write_profiles/pallas_call | solution.py:402
Async XLA Ops:
  0.6 0.7 %copy-start.2 = (s32[4,2]{0,1:T(2,128)S(1)}, s32[4,2]{0,1:T(2,128)}, u32[]{:S(2)}) copy-start(s32[4,2]{0,1:T(2,128)} %param.7) | copy-start | bytes 100
  0.6 0.7 %copy-start.3 = (s32[2]{0:T(128)S(1)}, s32[2]{0:T(128)}, u32[]{:S(2)}) copy-start(s32[2]{0:T(128)} %length_hbm.1) | copy-start | bytes 28
  1.3 0.7 %copy-start.1 = (f32[576]{0:T(1024)S(1)}, f32[576]{0:T(1024)}, u32[]{:S(2)}) copy-start(f32[576]{0:T(1024)} %series_ref.1) | copy-start | bytes 6916
  2.0 0.7 %copy-start.4 = (s32[2]{0:T(128)S(1)}, s32[2]{0:T(128)}, u32[]{:S(2)}) copy-start(s32[2]{0:T(128)} %barrier_hbm.1) | copy-start | bytes 28
  33.1 0.6 %copy-start = (f32[2,2,8,128]{3,2,1,0:T(8,128)}, f32[2,2,8,128]{3,2,1,0:T(8,128)S(1)}, u32[]{:S(2)}) copy-start(f32[2,2,8,128]{3,2,1,0:T(8,128)S(1)} %profile.1.groups_ref) | copy-start | bytes 49156
where the time goes:
time: 35.3 us; the launch traced here: 35 us
  Pallas kernels  31.8 us (90%)
  local copies, waits for them, and re-layouts  2.6 us (7%)
  between operations  0.67 us (2%)
    pallas_call x1, Pallas kernels, shards(): pl.pallas_call(functools.partial(profile_kernel, piece, n, count_len, len...  30.4 us
    unnamed x10, local copies, waits for them, and re-layouts  2.6 us
    pallas_call x1, Pallas kernels, shards(): pl.pallas_call(write_kernel, out_shape=(profile, profile), in_specs=[pl.B...  1.35 us

commit v1 on v0

--- a/solution.py
+++ b/solution.py
@@ -181,7 +181,7 @@
         load.wait()
 
     lengths = [length_ref[l] for l in range(count_len)]
-    row_ids = lax.broadcasted_iota(jnp.int32, (MAX_LEN, LANES), 0)
+    row_ids = lax.broadcasted_iota(jnp.int32, (MAX_LEN, 2 * LANES), 0)
     row_ids = row_ids + (SUBLANES - 1) - 2 * lax.rem(row_ids, SUBLANES)
     for l, length in enumerate(lengths):
         keep_ref[l] = jnp.where(row_ids < length, 1.0, 0.0).astype(jnp.bfloat16)
@@ -229,14 +229,17 @@
     def build(l, slot, buffer):
         firsts = [tile_ref[k, slot] * QUARTERS for k in range(2)]
         for k, (first, target) in enumerate(zip(firsts, (left_op, right_op))):
-            for u in range(QUARTERS):
-                centre, inverse = centre_ref[l, first + u], inverse_ref[l, first + u]
-                for c in range(MAX_LEN // LANES):
-                    rows = slice(c * LANES, (c + 1) * LANES)
-                    normal = ((base[first + u + c] - centre) * inverse).astype(jnp.bfloat16)
-                    if k == 0:
-                        normal = normal * keep_ref[l, rows, :]
-                    target[buffer, rows, u * LANES : (u + 1) * LANES] = normal
+            centre, inverse = (
+                jnp.concatenate([source[l, first + u] for u in range(QUARTERS)], axis=1)
+                for source in (centre_ref, inverse_ref)
+            )
+            for c in range(MAX_LEN // LANES):
+                rows = slice(c * LANES, (c + 1) * LANES)
+                values = jnp.concatenate([base[first + u + c] for u in range(QUARTERS)], axis=1)
+                normal = ((values - centre) * inverse).astype(jnp.bfloat16)
+                if k == 0:
+                    normal = normal * jnp.concatenate([keep_ref[l, rows, :]] * 2, axis=1)
+                target[buffer, rows, :] = normal
 
     def product(l, slot, buffer):
         row_block, col_block = tile_ref[0, slot], tile_ref[1, slot]
@@ -361,7 +364,7 @@
         functools.partial(
             profile_kernel, piece, n, count_len, len_devices, tile_list.shape[0]
         ),
-        out_shape=jax.ShapeDtypeStruct((len_devices, count_len, SUBLANES, LANES), jnp.float32),
+        out_shape=pltpu.VMEM((len_devices, count_len, SUBLANES, LANES), jnp.float32),
         in_specs=[pl.BlockSpec(memory_space=HBM)] * 4,
         out_specs=pl.BlockSpec(memory_space=VMEM),
         scratch_shapes=[
@@ -376,7 +379,7 @@
             pltpu.VMEM((columns, LANES, LANES), jnp.float32),
             pltpu.VMEM(depth, jnp.float32),
             pltpu.VMEM(depth, jnp.float32),
-            pltpu.VMEM((count_len, MAX_LEN, LANES), jnp.bfloat16),
+            pltpu.VMEM((count_len, MAX_LEN, 2 * LANES), jnp.bfloat16),
             pltpu.VMEM((2, MAX_LEN, TILE_SIDE), jnp.bfloat16),
             pltpu.VMEM((2, MAX_LEN, TILE_SIDE), jnp.bfloat16),
             pltpu.VMEM(minima, jnp.float32),
@@ -396,7 +399,12 @@
             vmem_limit_bytes=16 * GRANT + points * LANES * 4,
         ),
         name="profile",
-    )(series, tile_list.T, window_lengths, exclusion)
+    )(
+        *(
+            pltpu.with_memory_space_constraint(x, HBM)
+            for x in (series, tile_list.T, window_lengths, exclusion)
+        )
+    )
 
     profile = jax.ShapeDtypeStruct((len_devices * count_len, TILE_SIDE), jnp.float32)
     return pl.pallas_call(
@@ -409,6 +417,7 @@
             pltpu.VMEM(profile.shape, jnp.float32),
             dma((2,)),
         ],
+        compiler_params=pltpu.CompilerParams(vmem_limit_bytes=GRANT),
         name="write_profiles",
     )(groups)
 

time: 35.3 us -> 28.4 us (0.80)
  Pallas kernels: 31.8 us -> 27.6 us
  local copies, waits for them, and re-layouts: 2.6 us -> 0 us
    pallas_call x1, Pallas kernels: 30.4 us -> 26.9 us  [shards(): pl.pallas_call(functools.partial(profile_kernel, piece, n, count_len, len...]
    unnamed x10 -> x0, local copies, waits for them, and re-layouts: 2.6 us -> none
    pallas_call x1, Pallas kernels: 1.35 us -> 0.63 us  [shards(): pl.pallas_call(write_kernel, out_shape=(profile, profile), in_specs=[pl.B...]
where the time goes in v1:
time: 28.4 us; the launch traced here: 28.2 us
  Pallas kernels  27.6 us (97%)
  between operations  0.64 us (2%)
    pallas_call x1, Pallas kernels, shards(): pl.pallas_call(functools.partial(profile_kernel, piece, n, count_len, len...  26.9 us
    pallas_call x1, Pallas kernels, shards(): pl.pallas_call(write_kernel, out_shape=(profile, profile), in_specs=[pl.B...  0.63 us

profile of v1, /device:TPU:0, one launch (start us, length us, event | category | flops | bytes accessed | tf_op | source)
XLA Modules:
  0.0 28.2 jit_solution(1028624855166023529)
XLA Ops:
  0.6 26.9 %profile.1.groups_ref = f32[2,2,8,128]{3,2,1,0:T(8,128)S(1)} custom-call(f32[576]{0:T(1024)} %series_ref.1, s32[2,4]{1,0:T(2,128)} %bitcast.1, s32[2]{0:T(128)} %length_hbm.1, s32[2]{0:T(128)} %barrier_hbm.1), custom_call_target="tpu_custom_call" | custom-call | tf_op jit(solution)/shard_map/profile/pallas_call | solution.py:363
  27.6 0.6 %write_profiles.1 = (f32[4,512]{1,0:T(4,128)}, f32[4,512]{1,0:T(4,128)}) custom-call(f32[2,2,8,128]{3,2,1,0:T(8,128)S(1)} %profile.1.groups_ref), custom_call_target="tpu_custom_call" | custom-call | tf_op jit(solution)/shard_map/write_profiles/pallas_call | solution.py:410

commit v2 on v1

--- a/solution.py
+++ b/solution.py
@@ -14,6 +14,7 @@
 GRANT = 1 << 20
 QUARTERS = TILE_SIDE // LANES
 
+EMPTY_VALUE = 2.0
 VAR_EPS = 1e-05
 
 VMEM = pltpu.MemorySpace.VMEM
@@ -22,8 +23,6 @@
 
 
 def partner(me, step, n):
-    if n & (n - 1):
-        return lax.rem(me + step, n)
     peer = me
     for b in range(n.bit_length() - 1):
         if step >> b & 1:
@@ -31,28 +30,23 @@
     return peer
 
 
-def steps_of(n):
-    return range(n - 1, 0, -1)
-
-
 def signal_all(barrier, axis, n):
-    me = lax.axis_index(axis)
-    for step in range(1, n) if n & (n - 1) else steps_of(n):
+    for step in range(n - 1, 0, -1):
         pl.semaphore_signal(
             barrier,
             inc=1,
-            device_id={axis: partner(me, step, n)},
+            device_id={axis: partner(lax.axis_index(axis), step, n)},
             device_id_type=pl.DeviceIdType.MESH,
         )
 
 
-def copy_to(axis, n, step, source, target, send_sem, recv_sem):
+def copy_to(source, target, send_sem, recv_sem, **peer):
     return pltpu.make_async_remote_copy(
         src_ref=source,
         dst_ref=target,
         send_sem=send_sem,
         recv_sem=recv_sem,
-        device_id={axis: partner(lax.axis_index(axis), step, n)},
+        device_id=peer,
         device_id_type=pl.DeviceIdType.MESH,
     )
 
@@ -108,6 +102,8 @@
     n,
     count_len,
     len_devices,
+    planes,
+    chunk,
     slots_of_tiles,
     series_ref,
     tile_hbm,
@@ -121,6 +117,7 @@
     flat,
     staged,
     slots,
+    chunk_rows,
     packed,
     base,
     centre_ref,
@@ -141,6 +138,7 @@
 ):
     me = lax.axis_index("tile")
     my_len = lax.axis_index("len")
+    my_plane = my_len if planes > 1 else 0
     loads = [
         pltpu.make_async_copy(source, target, in_sem.at[k])
         for k, (source, target) in enumerate(
@@ -154,8 +152,20 @@
     ]
     loads[0].start()
     barrier = pltpu.get_barrier_semaphore()
-    signal_all(barrier, "tile", n)
-    signal_all(barrier, "len", len_devices)
+    for step in range(planes * n - 1, 0, -1):
+        pl.semaphore_signal(
+            barrier,
+            inc=1,
+            device_id={
+                "len": partner(my_len, step // n, len_devices),
+                "tile": partner(me, step % n, n),
+            },
+            device_id_type=pl.DeviceIdType.MESH,
+        )
+    greeted = planes * n - 1
+    if planes == 1:
+        signal_all(barrier, "len", len_devices)
+        greeted += len_devices - 1
     for load in loads[1:]:
         load.start()
 
@@ -169,12 +179,18 @@
     values = pltpu.roll(values, shift, 1)
     staged[...] = jnp.where(lane_ids >= shift, values, pltpu.roll(values, 1, 0))
 
-    pl.semaphore_wait(barrier, n - 1 + len_devices - 1)
-    copies = [
-        copy_to("tile", n, step, staged, slots.at[me], send_piece.at[step], recv_piece.at[step])
-        for step in steps_of(n)
-    ]
-    for copy in copies:
+    pl.semaphore_wait(barrier, greeted)
+    copies = {
+        step: copy_to(
+            staged,
+            slots.at[me],
+            send_piece.at[step],
+            recv_piece.at[step],
+            tile=partner(me, step, n),
+        )
+        for step in range(n - 1, 0, -1)
+    }
+    for copy in copies.values():
         copy.start()
     slots[me] = staged[...]
     for load in loads[1:]:
@@ -185,46 +201,52 @@
     row_ids = row_ids + (SUBLANES - 1) - 2 * lax.rem(row_ids, SUBLANES)
     for l, length in enumerate(lengths):
         keep_ref[l] = jnp.where(row_ids < length, 1.0, 0.0).astype(jnp.bfloat16)
-        best[l] = jnp.full(best.shape[1:], -length.astype(jnp.float32), jnp.float32)
-    packed[...] = jnp.zeros(packed.shape, jnp.float32)
-    for copy in copies:
-        copy.wait_recv()
-
+    best[...] = jnp.full(best.shape, EMPTY_VALUE, jnp.float32)
+
+    sub = lax.broadcasted_iota(jnp.int32, (SUBLANES, LANES), 0)
+    lane = lax.broadcasted_iota(jnp.int32, (SUBLANES, LANES), 1)
+    spans = [
+        (
+            LANES + 1 - SUBLANES * (g + 1),
+            slice(SUBLANES * g, SUBLANES * (g + 1)),
+            lane - sub < LANES + 1 - SUBLANES * (g + 1),
+        )
+        for g in range(LANES // SUBLANES)
+    ]
+    per = chunk * piece // LANES
+    chunks = n // chunk
+
+    def turn(row):
+        row = jnp.broadcast_to(row, (SUBLANES, LANES))
+        return [pltpu.roll(row, amount, 1, stride=1, stride_axis=0) for amount, _, _ in spans]
+
+    for k in range(chunks):
+        q = partner(lax.div(me, chunk), k, chunks)
+        for step in range(k * chunk, (k + 1) * chunk):
+            if step:
+                copies[step].wait_recv()
+        chunk_rows[q] = jnp.zeros(chunk_rows.shape[1:], jnp.float32)
+        for t in range(chunk):
+            low, first = divmod(t * piece, LANES)
+            used = (first + piece + LANES - 1) // LANES
+            chunk_rows[q, low : low + used, :] += slots[q * chunk + t, :used, :]
+        later = None
+        for j in range(per - 1, -1, -1):
+            moved = turn(chunk_rows[q, j : j + 1, :])
+            column = q * per + j + 1
+            for g, (_, rows, here) in enumerate(spans):
+                beyond = base[column, rows, :] if later is None else later[g]
+                base[column, rows, :] = jnp.where(here, moved[g], beyond)
+            later = moved
+        for g, (_, rows, here) in enumerate(spans):
+            base[q * per, rows, :] = jnp.where(here, base[q * per, rows, :], later[g])
+
+    for q in range(chunks):
+        packed[q * per : (q + 1) * per, :] = chunk_rows[q, :per, :]
     columns = packed.shape[0]
-    for t in range(n):
-        low, first = divmod(t * piece, LANES)
-        used = (first + piece + LANES - 1) // LANES
-        packed[low : low + used, :] += slots[t, :used, :]
-
     for l, (centre, inverse) in enumerate(window_stats(packed[...], lengths)):
         centre_ref[l] = centre.reshape(columns, 1, LANES)
         inverse_ref[l] = inverse.reshape(columns, 1, LANES)
-
-    sub = lax.broadcasted_iota(jnp.int32, (SUBLANES, LANES), 0)
-    lane = lax.broadcasted_iota(jnp.int32, (SUBLANES, LANES), 1)
-    groups8 = LANES // SUBLANES
-    span = 12 if columns % 12 == 0 else 1
-
-    def spread_columns(k, turned):
-        for j in range(span):
-            a = columns - 1 - k * span - j
-            row = jnp.broadcast_to(packed[pl.ds(a, 1), :], (SUBLANES, LANES))
-            later = []
-            for g in range(groups8):
-                moved = pltpu.roll(row, LANES + 1 - SUBLANES * (g + 1), 1, stride=1, stride_axis=0)
-                base[a, SUBLANES * g : SUBLANES * (g + 1), :] = jnp.where(
-                    lane - sub < LANES + 1 - SUBLANES * (g + 1), moved, turned[g]
-                )
-                later.append(moved)
-            turned = tuple(later)
-        return turned
-
-    lax.fori_loop(
-        0,
-        columns // span,
-        spread_columns,
-        (jnp.zeros((SUBLANES, LANES), jnp.float32),) * groups8,
-    )
 
     def build(l, slot, buffer):
         firsts = [tile_ref[k, slot] * QUARTERS for k in range(2)]
@@ -235,7 +257,9 @@
             )
             for c in range(MAX_LEN // LANES):
                 rows = slice(c * LANES, (c + 1) * LANES)
-                values = jnp.concatenate([base[first + u + c] for u in range(QUARTERS)], axis=1)
+                values = jnp.concatenate(
+                    [base[first + u + c + 1] for u in range(QUARTERS)], axis=1
+                )
                 normal = ((values - centre) * inverse).astype(jnp.bfloat16)
                 if k == 0:
                     normal = normal * jnp.concatenate([keep_ref[l, rows, :]] * 2, axis=1)
@@ -267,15 +291,32 @@
             for q in range(2):
                 turned_back = jnp.transpose(folded[q * LANES : (q + 1) * LANES, :])
                 found.append(jnp.max(turned_back, axis=0, keepdims=True))
-        both = jnp.full((SUBLANES, LANES), -size, jnp.float32)
-        for u in range(QUARTERS):
-            both = jnp.where(sub == u, found[u], both)
-            both = jnp.where(sub == QUARTERS + u, tops[u], both)
-        row_is, col_is = jnp.full(sub.shape, row_block), jnp.full(sub.shape, col_block)
-        owner = jnp.where(sub < QUARTERS, row_is, col_is)
+        both = jnp.broadcast_to(found[0], sub.shape)
+        for u, row in enumerate([*found[1:], *tops]):
+            both = jnp.where(sub == u + 1, row, both)
+        both = 1.0 - both / size
+        owner = jnp.where(
+            sub < QUARTERS, jnp.full(sub.shape, row_block), jnp.full(sub.shape, col_block)
+        )
         for b in range(n):
             old = best[l, b]
-            best[l, b] = jnp.where(owner == b, jnp.maximum(old, both), old)
+            best[l, b] = jnp.where(owner == b, jnp.minimum(old, both), old)
+
+    def send(l):
+        sent = [
+            copy_to(
+                best.at[l, partner(me, step % n, n)],
+                parts.at[my_plane, l, step % n],
+                send_sem.at[l, step],
+                recv_sem.at[l, step],
+                len=partner(my_len, step // n, len_devices),
+                tile=partner(me, step % n, n),
+            )
+            for step in sorted(range(1, planes * n), key=lambda s: (s % n, s), reverse=True)
+        ]
+        for copy in sent:
+            copy.start()
+        return sent
 
     sends = []
     work = [(l, slot) for l in range(count_len) for slot in range(slots_of_tiles)]
@@ -285,45 +326,41 @@
             build(*work[p + 1], (p + 1) % 2)
         product(l, slot, p % 2)
         if slot == slots_of_tiles - 1:
-            sends.append(
-                [
-                    copy_to(
-                        "tile",
-                        n,
-                        step,
-                        best.at[l, partner(me, step, n)],
-                        parts.at[l, step],
-                        send_sem.at[l, step],
-                        recv_sem.at[l, step],
-                    )
-                    for step in steps_of(n)
-                ]
-            )
-            for copy in sends[-1]:
-                copy.start()
+            sends.append(send(l))
+            parts[my_plane, l, 0] = best[l, me]
 
     for l in range(count_len):
         for copy in sends[l]:
             copy.wait_recv()
-        merged = best[l, me]
-        for step in range(1, n):
-            merged = jnp.maximum(merged, parts[l, step])
-        merged = 1.0 - merged / lengths[l].astype(jnp.float32)
-        mine[l] = merged
-        groups[my_len, l] = merged
-    copies_len = [
-        copy_to("len", len_devices, step, mine, groups.at[my_len], send_len.at[step], recv_len.at[step])
-        for step in range(1, len_devices)
-    ]
-    for copy in copies_len:
-        copy.start()
-    for copy in copies:
+        for g in range(planes):
+            merged = parts[g, l, 0]
+            for step in range(1, n):
+                merged = jnp.minimum(merged, parts[g, l, step])
+            if planes > 1:
+                groups[g, l] = merged
+            else:
+                mine[l] = merged
+                groups[my_len, l] = merged
+    if planes == 1:
+        hops = [
+            copy_to(
+                mine,
+                groups.at[my_len],
+                send_len.at[step],
+                recv_len.at[step],
+                len=partner(my_len, step, len_devices),
+            )
+            for step in range(1, len_devices)
+        ]
+        for copy in hops:
+            copy.start()
+        for copy in hops:
+            copy.wait()
+    for copy in copies.values():
         copy.wait_send()
-    for some in sends:
-        for copy in some:
+    for sent in sends:
+        for copy in sent:
             copy.wait_send()
-    for copy in copies_len:
-        copy.wait()
 
 
 def write_kernel(groups_ref, right_ref, left_ref, right, left, sems):
@@ -357,12 +394,23 @@
     slot_rows = (piece + 2 * LANES - 2) // LANES
     slot_rows = (slot_rows + SUBLANES - 1) // SUBLANES * SUBLANES
     depth = (count_len, columns, 1, LANES)
+    chunk = next(g for g in range(1, n + 1) if n % g == 0 and g * piece % LANES == 0)
+    per = chunk * piece // LANES
+    chunk_rows = (per + SUBLANES - 1) // SUBLANES * SUBLANES
+    planes = len_devices if len_devices <= 2 else 1
     minima = (count_len, n, SUBLANES, LANES)
     dma = pltpu.SemaphoreType.DMA
 
     groups = pl.pallas_call(
         functools.partial(
-            profile_kernel, piece, n, count_len, len_devices, tile_list.shape[0]
+            profile_kernel,
+            piece,
+            n,
+            count_len,
+            len_devices,
+            planes,
+            chunk,
+            tile_list.shape[0],
         ),
         out_shape=pltpu.VMEM((len_devices, count_len, SUBLANES, LANES), jnp.float32),
         in_specs=[pl.BlockSpec(memory_space=HBM)] * 4,
@@ -375,21 +423,22 @@
             pltpu.VMEM((slot_rows * LANES,), jnp.float32),
             pltpu.VMEM((slot_rows, LANES), jnp.float32),
             pltpu.VMEM((n, slot_rows, LANES), jnp.float32),
+            pltpu.VMEM((n // chunk, chunk_rows, LANES), jnp.float32),
             pltpu.VMEM((columns, LANES), jnp.float32),
-            pltpu.VMEM((columns, LANES, LANES), jnp.float32),
+            pltpu.VMEM((columns + 1, LANES, LANES), jnp.float32),
             pltpu.VMEM(depth, jnp.float32),
             pltpu.VMEM(depth, jnp.float32),
             pltpu.VMEM((count_len, MAX_LEN, 2 * LANES), jnp.bfloat16),
             pltpu.VMEM((2, MAX_LEN, TILE_SIDE), jnp.bfloat16),
             pltpu.VMEM((2, MAX_LEN, TILE_SIDE), jnp.bfloat16),
             pltpu.VMEM(minima, jnp.float32),
-            pltpu.VMEM(minima, jnp.float32),
+            pltpu.VMEM((planes, *minima), jnp.float32),
             pltpu.VMEM((count_len, SUBLANES, LANES), jnp.float32),
             dma((4,)),
             dma((n,)),
             dma((n,)),
-            dma((count_len, n)),
-            dma((count_len, n)),
+            dma((count_len, planes * n)),
+            dma((count_len, planes * n)),
             dma((len_devices,)),
             dma((len_devices,)),
         ],

time: 28.4 us -> 26.7 us (0.940)
  Pallas kernels: 27.6 us -> 25.9 us
    pallas_call x1, Pallas kernels: 26.9 us -> 25.3 us  [shards(): pl.pallas_call(functools.partial(profile_kernel, piece, n, count_len, len...]
where the time goes in v2:
time: 26.7 us; the launch traced here: 26.5 us
  Pallas kernels  25.9 us (97%)
  between operations  0.64 us (2%)
    pallas_call x1, Pallas kernels, shards(): pl.pallas_call(functools.partial(profile_kernel, piece, n, count_len, len...  25.3 us
    pallas_call x1, Pallas kernels, shards(): pl.pallas_call(write_kernel, out_shape=(profile, profile), in_specs=[pl.B...  0.63 us

profile of v2, /device:TPU:0, one launch (start us, length us, event | category | flops | bytes accessed | tf_op | source)
XLA Modules:
  0.0 26.5 jit_solution(9666123667288254360)
XLA Ops:
  0.6 25.3 %profile.1.groups_ref = f32[2,2,8,128]{3,2,1,0:T(8,128)S(1)} custom-call(f32[576]{0:T(1024)} %series_ref.1, s32[2,4]{1,0:T(2,128)} %bitcast.1, s32[2]{0:T(128)} %length_hbm.1, s32[2]{0:T(128)} %barrier_hbm.1), custom_call_target="tpu_custom_call" | custom-call | tf_op jit(solution)/shard_map/profile/pallas_call | solution.py:404
  25.9 0.6 %write_profiles.1 = (f32[4,512]{1,0:T(4,128)}, f32[4,512]{1,0:T(4,128)}) custom-call(f32[2,2,8,128]{3,2,1,0:T(8,128)S(1)} %profile.1.groups_ref), custom_call_target="tpu_custom_call" | custom-call | tf_op jit(solution)/shard_map/write_profiles/pallas_call | solution.py:459

commit v3 on v2

--- a/solution.py
+++ b/solution.py
@@ -104,7 +104,7 @@
     len_devices,
     planes,
     chunk,
-    slots_of_tiles,
+    deferred,
     series_ref,
     tile_hbm,
     length_hbm,
@@ -112,6 +112,7 @@
     groups,
     piece_ref,
     tile_ref,
+    tile_in,
     length_ref,
     barrier_ref,
     flat,
@@ -129,6 +130,9 @@
     parts,
     mine,
     in_sem,
+    tile_sem,
+    send_tile,
+    recv_tile,
     send_piece,
     recv_piece,
     send_sem,
@@ -144,7 +148,7 @@
         for k, (source, target) in enumerate(
             (
                 (series_ref, piece_ref),
-                (tile_hbm, tile_ref),
+                (tile_hbm, tile_ref.at[0]),
                 (length_hbm, length_ref),
                 (barrier_hbm, barrier_ref),
             )
@@ -192,16 +196,31 @@
     }
     for copy in copies.values():
         copy.start()
+    share = count_len
+    passed = [
+        copy_to(
+            tile_hbm,
+            tile_in.at[e],
+            send_tile.at[e],
+            recv_tile.at[e],
+            tile=partner(me, e, n),
+        )
+        for e in range(1, share)
+    ]
+    for copy in passed:
+        copy.start()
     slots[me] = staged[...]
     for load in loads[1:]:
         load.wait()
 
-    lengths = [length_ref[l] for l in range(count_len)]
+    turn_of_mine = lax.rem(me, share)
+    length, excluded = length_ref[turn_of_mine], barrier_ref[turn_of_mine]
+    size = length.astype(jnp.float32)
     row_ids = lax.broadcasted_iota(jnp.int32, (MAX_LEN, 2 * LANES), 0)
     row_ids = row_ids + (SUBLANES - 1) - 2 * lax.rem(row_ids, SUBLANES)
-    for l, length in enumerate(lengths):
-        keep_ref[l] = jnp.where(row_ids < length, 1.0, 0.0).astype(jnp.bfloat16)
-    best[...] = jnp.full(best.shape, EMPTY_VALUE, jnp.float32)
+    keep_ref[...] = jnp.where(row_ids < length, 1.0, 0.0).astype(jnp.bfloat16)
+    for ref in best:
+        ref[...] = jnp.full(ref.shape, EMPTY_VALUE, jnp.float32)
 
     sub = lax.broadcasted_iota(jnp.int32, (SUBLANES, LANES), 0)
     lane = lax.broadcasted_iota(jnp.int32, (SUBLANES, LANES), 1)
@@ -241,18 +260,31 @@
         for g, (_, rows, here) in enumerate(spans):
             base[q * per, rows, :] = jnp.where(here, base[q * per, rows, :], later[g])
 
+    for copy in passed:
+        copy.wait_recv()
+    moves = [
+        pltpu.make_async_copy(tile_in.at[e], tile_ref.at[e], tile_sem.at[e]) for e in range(1, share)
+    ]
+    for move in moves:
+        move.start()
     for q in range(chunks):
         packed[q * per : (q + 1) * per, :] = chunk_rows[q, :per, :]
     columns = packed.shape[0]
-    for l, (centre, inverse) in enumerate(window_stats(packed[...], lengths)):
-        centre_ref[l] = centre.reshape(columns, 1, LANES)
-        inverse_ref[l] = inverse.reshape(columns, 1, LANES)
-
-    def build(l, slot, buffer):
-        firsts = [tile_ref[k, slot] * QUARTERS for k in range(2)]
-        for k, (first, target) in enumerate(zip(firsts, (left_op, right_op))):
+    ((centre, inverse),) = window_stats(packed[...], [length])
+    centre_ref[...] = centre.reshape(columns, 1, LANES)
+    inverse_ref[...] = inverse.reshape(columns, 1, LANES)
+    for move in moves:
+        move.wait()
+
+    tiles = [(e, slot) for e in range(share) for slot in range(tile_ref.shape[2])]
+    blocks_of = [[tile_ref[e, k, slot] for k in range(2)] for e, slot in tiles]
+    half = TILE_SIDE // 2
+
+    def build(t):
+        for k, target in enumerate((left_op, right_op)):
+            first = blocks_of[t][k] * QUARTERS
             centre, inverse = (
-                jnp.concatenate([source[l, first + u] for u in range(QUARTERS)], axis=1)
+                jnp.concatenate([source[first + u] for u in range(QUARTERS)], axis=1)
                 for source in (centre_ref, inverse_ref)
             )
             for c in range(MAX_LEN // LANES):
@@ -262,53 +294,57 @@
                 )
                 normal = ((values - centre) * inverse).astype(jnp.bfloat16)
                 if k == 0:
-                    normal = normal * jnp.concatenate([keep_ref[l, rows, :]] * 2, axis=1)
-                target[buffer, rows, :] = normal
-
-    def product(l, slot, buffer):
-        row_block, col_block = tile_ref[0, slot], tile_ref[1, slot]
-        size = lengths[l].astype(jnp.float32)
-        limit = barrier_ref[l] - (col_block - row_block) * TILE_SIDE
-        tops = [None] * QUARTERS
-        found = []
-        for low in range(0, TILE_SIDE, 2 * LANES):
-            values = lax.dot_general(
-                left_op[buffer, :, low : low + 2 * LANES],
-                right_op[buffer],
-                (((0,), (0,)), ((), ())),
-                preferred_element_type=jnp.float32,
-            )
-            ahead = lax.broadcasted_iota(jnp.int32, values.shape, 1) - (
-                lax.broadcasted_iota(jnp.int32, values.shape, 0) + low
-            )
-            values = jnp.where(ahead > limit, values, -size)
-            folded = None
-            for u in range(QUARTERS):
-                part = values[:, u * LANES : (u + 1) * LANES]
-                folded = part if folded is None else jnp.maximum(folded, part)
-                top = jnp.max(part, axis=0, keepdims=True)
-                tops[u] = top if tops[u] is None else jnp.maximum(tops[u], top)
-            for q in range(2):
-                turned_back = jnp.transpose(folded[q * LANES : (q + 1) * LANES, :])
-                found.append(jnp.max(turned_back, axis=0, keepdims=True))
-        both = jnp.broadcast_to(found[0], sub.shape)
-        for u, row in enumerate([*found[1:], *tops]):
-            both = jnp.where(sub == u + 1, row, both)
-        both = 1.0 - both / size
+                    normal = normal * jnp.concatenate([keep_ref[rows, :]] * 2, axis=1)
+                target[t, rows, :] = normal
+
+    def product(t, row, col, width):
+        row_block, col_block = blocks_of[t]
+        limit = excluded - (col_block - row_block) * TILE_SIDE
+        values = lax.dot_general(
+            left_op[t, :, row : row + half],
+            right_op[t, :, col : col + width],
+            (((0,), (0,)), ((), ())),
+            preferred_element_type=jnp.float32,
+        )
+        ahead = (lax.broadcasted_iota(jnp.int32, values.shape, 1) + col) - (
+            lax.broadcasted_iota(jnp.int32, values.shape, 0) + row
+        )
+        values = jnp.where(ahead > limit, values, -size)
+        folded, tops = None, []
+        for u in range(0, width, LANES):
+            part = values[:, u : u + LANES]
+            folded = part if folded is None else jnp.maximum(folded, part)
+            tops.append(jnp.max(part, axis=0, keepdims=True))
+        found = [
+            jnp.max(jnp.transpose(folded[u : u + LANES, :]), axis=0, keepdims=True)
+            for u in range(0, half, LANES)
+        ]
+        return found, tops
+
+    def larger(some, others):
+        return [jnp.maximum(x, y) for x, y in zip(some, others)]
+
+    def update(r, t, right, left):
+        row_block, col_block = blocks_of[t]
+        ref = best[r]
+        lines = lax.broadcasted_iota(jnp.int32, ref.shape[1:], 0)
+        found = jnp.broadcast_to((right + left)[0], ref.shape[1:])
+        for u, line in enumerate((right + left)[1:]):
+            found = jnp.where(lines == u + 1, line, found)
+        found = 1.0 - found / size
         owner = jnp.where(
-            sub < QUARTERS, jnp.full(sub.shape, row_block), jnp.full(sub.shape, col_block)
+            lines < len(right), jnp.full(lines.shape, row_block), jnp.full(lines.shape, col_block)
         )
         for b in range(n):
-            old = best[l, b]
-            best[l, b] = jnp.where(owner == b, jnp.minimum(old, both), old)
-
-    def send(l):
+            ref[b] = jnp.minimum(ref[b], jnp.where(owner == b, found, EMPTY_VALUE))
+
+    def send(r):
         sent = [
             copy_to(
-                best.at[l, partner(me, step % n, n)],
-                parts.at[my_plane, l, step % n],
-                send_sem.at[l, step],
-                recv_sem.at[l, step],
+                best[r].at[partner(me, step % n, n)],
+                parts[r].at[my_plane, step % n],
+                send_sem.at[r, step],
+                recv_sem.at[r, step],
                 len=partner(my_len, step // n, len_devices),
                 tile=partner(me, step % n, n),
             )
@@ -316,31 +352,49 @@
         ]
         for copy in sent:
             copy.start()
+        parts[r][my_plane, 0] = best[r][me]
         return sent
 
-    sends = []
-    work = [(l, slot) for l in range(count_len) for slot in range(slots_of_tiles)]
-    build(*work[0], 0)
-    for p, (l, slot) in enumerate(work):
-        if p + 1 < len(work):
-            build(*work[p + 1], (p + 1) % 2)
-        product(l, slot, p % 2)
-        if slot == slots_of_tiles - 1:
-            sends.append(send(l))
-            parts[my_plane, l, 0] = best[l, me]
-
-    for l in range(count_len):
-        for copy in sends[l]:
+    late = range(len(tiles) - deferred, len(tiles))
+    tops_of, found_of = {}, {}
+    build(0)
+    for t in range(len(tiles)):
+        if t + 1 < len(tiles):
+            build(t + 1)
+        found, tops_of[t] = product(t, 0, 0, TILE_SIDE)
+        update(0, t, found, [])
+        if t not in late:
+            found, tops = product(t, half, 0, TILE_SIDE)
+            tops = larger(tops, tops_of[t])
+            update(1, t, [], tops[:2])
+            update(2, t, found, tops[2:])
+    sends = [send(0)]
+    for t in late:
+        found_of[t], tops = product(t, half, 0, half)
+        update(1, t, [], larger(tops, tops_of[t][:2]))
+    sends.append(send(1))
+    for t in late:
+        found, tops = product(t, half, half, half)
+        update(2, t, larger(found, found_of[t]), larger(tops, tops_of[t][2:]))
+    sends.append(send(2))
+
+    filled = 0
+    for r, ref in enumerate(parts):
+        for copy in sends[r]:
             copy.wait_recv()
+        lines = slice(filled, filled + ref.shape[2])
+        filled += ref.shape[2]
         for g in range(planes):
-            merged = parts[g, l, 0]
-            for step in range(1, n):
-                merged = jnp.minimum(merged, parts[g, l, step])
-            if planes > 1:
-                groups[g, l] = merged
-            else:
-                mine[l] = merged
-                groups[my_len, l] = merged
+            for e in range(share):
+                merged = ref[g, e]
+                for step in range(e + share, n, share):
+                    merged = jnp.minimum(merged, ref[g, step])
+                l = partner(turn_of_mine, e, share)
+                if planes > 1:
+                    groups[g, l, lines, :] = merged
+                else:
+                    mine[l, lines, :] = merged
+                    groups[my_len, l, lines, :] = merged
     if planes == 1:
         hops = [
             copy_to(
@@ -356,7 +410,7 @@
             copy.start()
         for copy in hops:
             copy.wait()
-    for copy in copies.values():
+    for copy in [*copies.values(), *passed]:
         copy.wait_send()
     for sent in sends:
         for copy in sent:
@@ -370,8 +424,9 @@
             row = g * count_len + l
             for u in range(QUARTERS):
                 lanes = slice(u * LANES, (u + 1) * LANES)
-                right[row : row + 1, lanes] = groups_ref[g, l, u : u + 1, :]
-                left[row : row + 1, lanes] = groups_ref[g, l, QUARTERS + u : QUARTERS + u + 1, :]
+                line = u + u // 2 * 2
+                right[row : row + 1, lanes] = groups_ref[g, l, line : line + 1, :]
+                left[row : row + 1, lanes] = groups_ref[g, l, line + 2 : line + 3, :]
     copies = [
         pltpu.make_async_copy(right, right_ref, sems.at[0]),
         pltpu.make_async_copy(left, left_ref, sems.at[1]),
@@ -393,12 +448,14 @@
     assert blocks == n
     slot_rows = (piece + 2 * LANES - 2) // LANES
     slot_rows = (slot_rows + SUBLANES - 1) // SUBLANES * SUBLANES
-    depth = (count_len, columns, 1, LANES)
+    depth = (columns, 1, LANES)
     chunk = next(g for g in range(1, n + 1) if n % g == 0 and g * piece % LANES == 0)
     per = chunk * piece // LANES
     chunk_rows = (per + SUBLANES - 1) // SUBLANES * SUBLANES
     planes = len_devices if len_devices <= 2 else 1
-    minima = (count_len, n, SUBLANES, LANES)
+    share = count_len
+    assert n % share == 0 and share & (share - 1) == 0
+    rounds = (2, 2, 4)
     dma = pltpu.SemaphoreType.DMA
 
     groups = pl.pallas_call(
@@ -410,14 +467,15 @@
             len_devices,
             planes,
             chunk,
-            tile_list.shape[0],
+            share * tile_list.shape[0] // 2,
         ),
         out_shape=pltpu.VMEM((len_devices, count_len, SUBLANES, LANES), jnp.float32),
         in_specs=[pl.BlockSpec(memory_space=HBM)] * 4,
         out_specs=pl.BlockSpec(memory_space=VMEM),
         scratch_shapes=[
             pltpu.VMEM((piece,), jnp.float32),
-            pltpu.SMEM(tile_list.shape[::-1], jnp.int32),
+            pltpu.SMEM((share, *tile_list.shape[::-1]), jnp.int32),
+            pltpu.VMEM((share, *tile_list.shape[::-1]), jnp.int32),
             pltpu.SMEM(window_lengths.shape, jnp.int32),
             pltpu.SMEM(exclusion.shape, jnp.int32),
             pltpu.VMEM((slot_rows * LANES,), jnp.float32),
@@ -428,24 +486,27 @@
             pltpu.VMEM((columns + 1, LANES, LANES), jnp.float32),
             pltpu.VMEM(depth, jnp.float32),
             pltpu.VMEM(depth, jnp.float32),
-            pltpu.VMEM((count_len, MAX_LEN, 2 * LANES), jnp.bfloat16),
-            pltpu.VMEM((2, MAX_LEN, TILE_SIDE), jnp.bfloat16),
-            pltpu.VMEM((2, MAX_LEN, TILE_SIDE), jnp.bfloat16),
-            pltpu.VMEM(minima, jnp.float32),
-            pltpu.VMEM((planes, *minima), jnp.float32),
+            pltpu.VMEM((MAX_LEN, 2 * LANES), jnp.bfloat16),
+            pltpu.VMEM((share * tile_list.shape[0], MAX_LEN, TILE_SIDE), jnp.bfloat16),
+            pltpu.VMEM((share * tile_list.shape[0], MAX_LEN, TILE_SIDE), jnp.bfloat16),
+            tuple(pltpu.VMEM((n, lines, LANES), jnp.float32) for lines in rounds),
+            tuple(pltpu.VMEM((planes, n, lines, LANES), jnp.float32) for lines in rounds),
             pltpu.VMEM((count_len, SUBLANES, LANES), jnp.float32),
             dma((4,)),
+            dma((share,)),
+            dma((share,)),
+            dma((share,)),
             dma((n,)),
             dma((n,)),
-            dma((count_len, planes * n)),
-            dma((count_len, planes * n)),
+            dma((len(rounds), planes * n)),
+            dma((len(rounds), planes * n)),
             dma((len_devices,)),
             dma((len_devices,)),
         ],
         compiler_params=pltpu.CompilerParams(
             collective_id=0,
             has_side_effects=True,
-            vmem_limit_bytes=16 * GRANT + points * LANES * 4,
+            vmem_limit_bytes=28 * GRANT + points * LANES * 4,
         ),
         name="profile",
     )(

time: 26.7 us -> 27.5 us (1.030)
  Pallas kernels: 25.9 us -> 26.7 us
    pallas_call x1, Pallas kernels: 25.3 us -> 26 us  [shards(): pl.pallas_call(functools.partial(profile_kernel, piece, n, count_len, len...]
where the time goes in v3:
time: 27.5 us; the launch traced here: 27.3 us
  Pallas kernels  26.7 us (97%)
  between operations  0.64 us (2%)
    pallas_call x1, Pallas kernels, shards(): pl.pallas_call(functools.partial(profile_kernel, piece, n, count_len, len...  26 us
    pallas_call x1, Pallas kernels, shards(): pl.pallas_call(write_kernel, out_shape=(profile, profile), in_specs=[pl.B...  0.63 us

profile of v3, /device:TPU:0, one launch (start us, length us, event | category | flops | bytes accessed | tf_op | source)
XLA Modules:
  0.0 27.3 jit_solution(11933197472969739242)
XLA Ops:
  0.6 26.0 %profile.1.groups_ref = f32[2,2,8,128]{3,2,1,0:T(8,128)S(1)} custom-call(f32[576]{0:T(1024)} %series_ref.1, s32[2,4]{1,0:T(2,128)} %bitcast.1, s32[2]{0:T(128)} %length_hbm.1, s32[2]{0:T(128)} %barrier_hbm.1), custom_call_target="tpu_custom_call" | custom-call | tf_op jit(solution)/shard_map/profile/pallas_call | solution.py:461
  26.7 0.6 %write_profiles.1 = (f32[4,512]{1,0:T(4,128)}, f32[4,512]{1,0:T(4,128)}) custom-call(f32[2,2,8,128]{3,2,1,0:T(8,128)S(1)} %profile.1.groups_ref), custom_call_target="tpu_custom_call" | custom-call | tf_op jit(solution)/shard_map/write_profiles/pallas_call | solution.py:520

commit v4 on v2

--- a/solution.py
+++ b/solution.py
@@ -38,6 +38,11 @@
             device_id={axis: partner(lax.axis_index(axis), step, n)},
             device_id_type=pl.DeviceIdType.MESH,
         )
+
+
+def await_all(ref, sem, sent):
+    copy = copy_to(ref, ref, sem, sem)
+    copy.wait_send() if sent else copy.wait_recv()
 
 
 def copy_to(source, target, send_sem, recv_sem, **peer):
@@ -104,7 +109,6 @@
     len_devices,
     planes,
     chunk,
-    slots_of_tiles,
     series_ref,
     tile_hbm,
     length_hbm,
@@ -129,6 +133,9 @@
     parts,
     mine,
     in_sem,
+    send_tile,
+    recv_tile,
+    plane_sem,
     send_piece,
     recv_piece,
     send_sem,
@@ -144,7 +151,7 @@
         for k, (source, target) in enumerate(
             (
                 (series_ref, piece_ref),
-                (tile_hbm, tile_ref),
+                (tile_hbm, tile_ref.at[0]),
                 (length_hbm, length_ref),
                 (barrier_hbm, barrier_ref),
             )
@@ -152,20 +159,8 @@
     ]
     loads[0].start()
     barrier = pltpu.get_barrier_semaphore()
-    for step in range(planes * n - 1, 0, -1):
-        pl.semaphore_signal(
-            barrier,
-            inc=1,
-            device_id={
-                "len": partner(my_len, step // n, len_devices),
-                "tile": partner(me, step % n, n),
-            },
-            device_id_type=pl.DeviceIdType.MESH,
-        )
-    greeted = planes * n - 1
-    if planes == 1:
-        signal_all(barrier, "len", len_devices)
-        greeted += len_devices - 1
+    signal_all(barrier, "tile", n)
+    signal_all(barrier, "len", len_devices)
     for load in loads[1:]:
         load.start()
 
@@ -179,28 +174,46 @@
     values = pltpu.roll(values, shift, 1)
     staged[...] = jnp.where(lane_ids >= shift, values, pltpu.roll(values, 1, 0))
 
-    pl.semaphore_wait(barrier, greeted)
-    copies = {
-        step: copy_to(
+    pl.semaphore_wait(barrier, n - 1 + len_devices - 1)
+    for step in range(n - 1, 0, -1):
+        copy_to(
             staged,
             slots.at[me],
-            send_piece.at[step],
-            recv_piece.at[step],
+            send_piece,
+            recv_piece.at[step // chunk],
             tile=partner(me, step, n),
-        )
-        for step in range(n - 1, 0, -1)
-    }
-    for copy in copies.values():
-        copy.start()
+        ).start()
+    if planes > 1:
+        for step in range(1, len_devices):
+            pl.semaphore_signal(
+                plane_sem,
+                inc=1,
+                device_id={"len": partner(my_len, step, len_devices)},
+                device_id_type=pl.DeviceIdType.MESH,
+            )
     slots[me] = staged[...]
     for load in loads[1:]:
         load.wait()
-
-    lengths = [length_ref[l] for l in range(count_len)]
+    share = count_len
+    passed = [
+        copy_to(
+            tile_ref.at[0],
+            tile_ref.at[e],
+            send_tile.at[e],
+            recv_tile.at[e],
+            tile=partner(me, e, n),
+        )
+        for e in range(1, share)
+    ]
+    for copy in passed:
+        copy.start()
+
+    turn_of_mine = lax.rem(me, share)
+    length, excluded = length_ref[turn_of_mine], barrier_ref[turn_of_mine]
+    size = length.astype(jnp.float32)
     row_ids = lax.broadcasted_iota(jnp.int32, (MAX_LEN, 2 * LANES), 0)
     row_ids = row_ids + (SUBLANES - 1) - 2 * lax.rem(row_ids, SUBLANES)
-    for l, length in enumerate(lengths):
-        keep_ref[l] = jnp.where(row_ids < length, 1.0, 0.0).astype(jnp.bfloat16)
+    keep_ref[...] = jnp.where(row_ids < length, 1.0, 0.0).astype(jnp.bfloat16)
     best[...] = jnp.full(best.shape, EMPTY_VALUE, jnp.float32)
 
     sub = lax.broadcasted_iota(jnp.int32, (SUBLANES, LANES), 0)
@@ -218,13 +231,14 @@
 
     def turn(row):
         row = jnp.broadcast_to(row, (SUBLANES, LANES))
-        return [pltpu.roll(row, amount, 1, stride=1, stride_axis=0) for amount, _, _ in spans]
+        row = pltpu.roll(row, LANES + 1 - SUBLANES, 1, stride=1, stride_axis=0)
+        return [row] + [pltpu.roll(row, LANES - SUBLANES * g, 1) for g in range(1, len(spans))]
 
     for k in range(chunks):
         q = partner(lax.div(me, chunk), k, chunks)
-        for step in range(k * chunk, (k + 1) * chunk):
-            if step:
-                copies[step].wait_recv()
+        coming = chunk if k else chunk - 1
+        if coming:
+            await_all(slots.at[pl.ds(0, coming)], recv_piece.at[k], False)
         chunk_rows[q] = jnp.zeros(chunk_rows.shape[1:], jnp.float32)
         for t in range(chunk):
             low, first = divmod(t * piece, LANES)
@@ -241,18 +255,24 @@
         for g, (_, rows, here) in enumerate(spans):
             base[q * per, rows, :] = jnp.where(here, base[q * per, rows, :], later[g])
 
+    for copy in passed:
+        copy.wait()
+    await_all(slots.at[pl.ds(0, n - 1)], send_piece, True)
     for q in range(chunks):
         packed[q * per : (q + 1) * per, :] = chunk_rows[q, :per, :]
     columns = packed.shape[0]
-    for l, (centre, inverse) in enumerate(window_stats(packed[...], lengths)):
-        centre_ref[l] = centre.reshape(columns, 1, LANES)
-        inverse_ref[l] = inverse.reshape(columns, 1, LANES)
-
-    def build(l, slot, buffer):
-        firsts = [tile_ref[k, slot] * QUARTERS for k in range(2)]
-        for k, (first, target) in enumerate(zip(firsts, (left_op, right_op))):
+    ((centre, inverse),) = window_stats(packed[...], [length])
+    centre_ref[...] = centre.reshape(columns, 1, LANES)
+    inverse_ref[...] = inverse.reshape(columns, 1, LANES)
+
+    tiles = [(e, slot) for e in range(share) for slot in range(tile_ref.shape[2])]
+    blocks_of = [[tile_ref[e, k, slot] for k in range(2)] for e, slot in tiles]
+
+    def build(t):
+        for k, target in enumerate((left_op, right_op)):
+            first = blocks_of[t][k] * QUARTERS
             centre, inverse = (
-                jnp.concatenate([source[l, first + u] for u in range(QUARTERS)], axis=1)
+                jnp.concatenate([source[first + u] for u in range(QUARTERS)], axis=1)
                 for source in (centre_ref, inverse_ref)
             )
             for c in range(MAX_LEN // LANES):
@@ -262,19 +282,17 @@
                 )
                 normal = ((values - centre) * inverse).astype(jnp.bfloat16)
                 if k == 0:
-                    normal = normal * jnp.concatenate([keep_ref[l, rows, :]] * 2, axis=1)
-                target[buffer, rows, :] = normal
-
-    def product(l, slot, buffer):
-        row_block, col_block = tile_ref[0, slot], tile_ref[1, slot]
-        size = lengths[l].astype(jnp.float32)
-        limit = barrier_ref[l] - (col_block - row_block) * TILE_SIDE
-        tops = [None] * QUARTERS
-        found = []
+                    normal = normal * jnp.concatenate([keep_ref[rows, :]] * 2, axis=1)
+                target[t, rows, :] = normal
+
+    def product(t):
+        row_block, col_block = blocks_of[t]
+        limit = excluded - (col_block - row_block) * TILE_SIDE
+        tops, found = [None] * QUARTERS, []
         for low in range(0, TILE_SIDE, 2 * LANES):
             values = lax.dot_general(
-                left_op[buffer, :, low : low + 2 * LANES],
-                right_op[buffer],
+                left_op[t, :, low : low + 2 * LANES],
+                right_op[t],
                 (((0,), (0,)), ((), ())),
                 preferred_element_type=jnp.float32,
             )
@@ -299,43 +317,35 @@
             sub < QUARTERS, jnp.full(sub.shape, row_block), jnp.full(sub.shape, col_block)
         )
         for b in range(n):
-            old = best[l, b]
-            best[l, b] = jnp.where(owner == b, jnp.minimum(old, both), old)
-
-    def send(l):
-        sent = [
-            copy_to(
-                best.at[l, partner(me, step % n, n)],
-                parts.at[my_plane, l, step % n],
-                send_sem.at[l, step],
-                recv_sem.at[l, step],
-                len=partner(my_len, step // n, len_devices),
-                tile=partner(me, step % n, n),
-            )
-            for step in sorted(range(1, planes * n), key=lambda s: (s % n, s), reverse=True)
-        ]
-        for copy in sent:
-            copy.start()
-        return sent
-
-    sends = []
-    work = [(l, slot) for l in range(count_len) for slot in range(slots_of_tiles)]
-    build(*work[0], 0)
-    for p, (l, slot) in enumerate(work):
-        if p + 1 < len(work):
-            build(*work[p + 1], (p + 1) % 2)
-        product(l, slot, p % 2)
-        if slot == slots_of_tiles - 1:
-            sends.append(send(l))
-            parts[my_plane, l, 0] = best[l, me]
-
-    for l in range(count_len):
-        for copy in sends[l]:
-            copy.wait_recv()
-        for g in range(planes):
-            merged = parts[g, l, 0]
-            for step in range(1, n):
-                merged = jnp.minimum(merged, parts[g, l, step])
+            best[b] = jnp.minimum(best[b], jnp.where(owner == b, both, EMPTY_VALUE))
+
+    build(0)
+    for t in range(len(tiles)):
+        if t + 1 < len(tiles):
+            build(t + 1)
+        product(t)
+
+    if planes > 1:
+        pl.semaphore_wait(plane_sem, len_devices - 1)
+    for step in sorted(range(1, planes * n), key=lambda s: (s % n, s), reverse=True):
+        copy_to(
+            best.at[partner(me, step % n, n)],
+            parts.at[my_plane * n + step % n],
+            send_sem,
+            recv_sem,
+            len=partner(my_len, step // n, len_devices),
+            tile=partner(me, step % n, n),
+        ).start()
+    parts[my_plane * n] = best[me]
+    everyone = parts.at[pl.ds(0, planes * n - 1)]
+    await_all(everyone, send_sem, True)
+    await_all(everyone, recv_sem, False)
+    for g in range(planes):
+        for e in range(share):
+            merged = parts[g * n + e]
+            for step in range(e + share, n, share):
+                merged = jnp.minimum(merged, parts[g * n + step])
+            l = partner(turn_of_mine, e, share)
             if planes > 1:
                 groups[g, l] = merged
             else:
@@ -356,11 +366,6 @@
             copy.start()
         for copy in hops:
             copy.wait()
-    for copy in copies.values():
-        copy.wait_send()
-    for sent in sends:
-        for copy in sent:
-            copy.wait_send()
 
 
 def write_kernel(groups_ref, right_ref, left_ref, right, left, sems):
@@ -393,12 +398,13 @@
     assert blocks == n
     slot_rows = (piece + 2 * LANES - 2) // LANES
     slot_rows = (slot_rows + SUBLANES - 1) // SUBLANES * SUBLANES
-    depth = (count_len, columns, 1, LANES)
+    depth = (columns, 1, LANES)
     chunk = next(g for g in range(1, n + 1) if n % g == 0 and g * piece % LANES == 0)
     per = chunk * piece // LANES
     chunk_rows = (per + SUBLANES - 1) // SUBLANES * SUBLANES
     planes = len_devices if len_devices <= 2 else 1
-    minima = (count_len, n, SUBLANES, LANES)
+    share = count_len
+    assert n % share == 0 and share & (share - 1) == 0
     dma = pltpu.SemaphoreType.DMA
 
     groups = pl.pallas_call(
@@ -410,14 +416,13 @@
             len_devices,
             planes,
             chunk,
-            tile_list.shape[0],
         ),
         out_shape=pltpu.VMEM((len_devices, count_len, SUBLANES, LANES), jnp.float32),
         in_specs=[pl.BlockSpec(memory_space=HBM)] * 4,
         out_specs=pl.BlockSpec(memory_space=VMEM),
         scratch_shapes=[
             pltpu.VMEM((piece,), jnp.float32),
-            pltpu.SMEM(tile_list.shape[::-1], jnp.int32),
+            pltpu.SMEM((share, *tile_list.shape[::-1]), jnp.int32),
             pltpu.SMEM(window_lengths.shape, jnp.int32),
             pltpu.SMEM(exclusion.shape, jnp.int32),
             pltpu.VMEM((slot_rows * LANES,), jnp.float32),
@@ -428,24 +433,27 @@
             pltpu.VMEM((columns + 1, LANES, LANES), jnp.float32),
             pltpu.VMEM(depth, jnp.float32),
             pltpu.VMEM(depth, jnp.float32),
-            pltpu.VMEM((count_len, MAX_LEN, 2 * LANES), jnp.bfloat16),
-            pltpu.VMEM((2, MAX_LEN, TILE_SIDE), jnp.bfloat16),
-            pltpu.VMEM((2, MAX_LEN, TILE_SIDE), jnp.bfloat16),
-            pltpu.VMEM(minima, jnp.float32),
-            pltpu.VMEM((planes, *minima), jnp.float32),
+            pltpu.VMEM((MAX_LEN, 2 * LANES), jnp.bfloat16),
+            pltpu.VMEM((share * tile_list.shape[0], MAX_LEN, TILE_SIDE), jnp.bfloat16),
+            pltpu.VMEM((share * tile_list.shape[0], MAX_LEN, TILE_SIDE), jnp.bfloat16),
+            pltpu.VMEM((n, SUBLANES, LANES), jnp.float32),
+            pltpu.VMEM((planes * n, SUBLANES, LANES), jnp.float32),
             pltpu.VMEM((count_len, SUBLANES, LANES), jnp.float32),
             dma((4,)),
-            dma((n,)),
-            dma((n,)),
-            dma((count_len, planes * n)),
-            dma((count_len, planes * n)),
+            dma((share,)),
+            dma((share,)),
+            pltpu.SemaphoreType.REGULAR,
+            dma,
+            dma((n // chunk,)),
+            dma,
+            dma,
             dma((len_devices,)),
             dma((len_devices,)),
         ],
         compiler_params=pltpu.CompilerParams(
             collective_id=0,
             has_side_effects=True,
-            vmem_limit_bytes=16 * GRANT + points * LANES * 4,
+            vmem_limit_bytes=28 * GRANT + points * LANES * 4,
         ),
         name="profile",
     )(

time: 26.7 us -> 25.4 us (0.951)
  Pallas kernels: 25.9 us -> 24.6 us
    pallas_call x1, Pallas kernels: 25.3 us -> 23.9 us  [shards(): pl.pallas_call(functools.partial(profile_kernel, piece, n, count_len, len...]
where the time goes in v4:
time: 25.4 us; the launch traced here: 25.2 us
  Pallas kernels  24.6 us (97%)
  between operations  0.64 us (3%)
    pallas_call x1, Pallas kernels, shards(): pl.pallas_call(functools.partial(profile_kernel, piece, n, count_len, len...  23.9 us
    pallas_call x1, Pallas kernels, shards(): pl.pallas_call(write_kernel, out_shape=(profile, profile), in_specs=[pl.B...  0.63 us

profile of v4, /device:TPU:0, one launch (start us, length us, event | category | flops | bytes accessed | tf_op | source)
XLA Modules:
  0.0 25.2 jit_solution(6056042428798331783)
XLA Ops:
  0.6 23.9 %profile.1.groups_ref = f32[2,2,8,128]{3,2,1,0:T(8,128)S(1)} custom-call(f32[576]{0:T(1024)} %series_ref.1, s32[2,4]{1,0:T(2,128)} %bitcast.1, s32[2]{0:T(128)} %length_hbm.1, s32[2]{0:T(128)} %barrier_hbm.1), custom_call_target="tpu_custom_call" | custom-call | tf_op jit(solution)/shard_map/profile/pallas_call | solution.py:410
  24.6 0.6 %write_profiles.1 = (f32[4,512]{1,0:T(4,128)}, f32[4,512]{1,0:T(4,128)}) custom-call(f32[2,2,8,128]{3,2,1,0:T(8,128)S(1)} %profile.1.groups_ref), custom_call_target="tpu_custom_call" | custom-call | tf_op jit(solution)/shard_map/write_profiles/pallas_call | solution.py:467

commit v5 on v4

--- a/solution.py
+++ b/solution.py
@@ -15,6 +15,7 @@
 QUARTERS = TILE_SIDE // LANES
 
 EMPTY_VALUE = 2.0
+CLOSED = -1e30
 VAR_EPS = 1e-05
 
 VMEM = pltpu.MemorySpace.VMEM
@@ -127,6 +128,7 @@
     centre_ref,
     inverse_ref,
     keep_ref,
+    bound_ref,
     left_op,
     right_op,
     best,
@@ -211,10 +213,19 @@
     turn_of_mine = lax.rem(me, share)
     length, excluded = length_ref[turn_of_mine], barrier_ref[turn_of_mine]
     size = length.astype(jnp.float32)
-    row_ids = lax.broadcasted_iota(jnp.int32, (MAX_LEN, 2 * LANES), 0)
+    parts_of = MAX_LEN // LANES
+    last = lax.div(length - 1, LANES)
+    order = [lax.rem(last + 1 + c, parts_of) for c in range(parts_of)]
+    row_ids = lax.broadcasted_iota(jnp.int32, (LANES, 2 * LANES), 0)
     row_ids = row_ids + (SUBLANES - 1) - 2 * lax.rem(row_ids, SUBLANES)
-    keep_ref[...] = jnp.where(row_ids < length, 1.0, 0.0).astype(jnp.bfloat16)
+    keep_ref[...] = jnp.where(row_ids < length - last * LANES, 1.0, 0.0).astype(jnp.bfloat16)
     best[...] = jnp.full(best.shape, EMPTY_VALUE, jnp.float32)
+    lane_less_sub = lax.broadcasted_iota(jnp.int32, (SUBLANES, LANES), 1) - lax.broadcasted_iota(
+        jnp.int32, (SUBLANES, LANES), 0
+    )
+    for e in range(bound_ref.shape[0]):
+        open_here = lane_less_sub > excluded + (TILE_SIDE - SUBLANES - e * SUBLANES)
+        bound_ref[e] = jnp.where(open_here, -CLOSED, CLOSED)
 
     sub = lax.broadcasted_iota(jnp.int32, (SUBLANES, LANES), 0)
     lane = lax.broadcasted_iota(jnp.int32, (SUBLANES, LANES), 1)
@@ -268,6 +279,8 @@
     tiles = [(e, slot) for e in range(share) for slot in range(tile_ref.shape[2])]
     blocks_of = [[tile_ref[e, k, slot] for k in range(2)] for e, slot in tiles]
 
+    gates = {}
+
     def build(t):
         for k, target in enumerate((left_op, right_op)):
             first = blocks_of[t][k] * QUARTERS
@@ -275,19 +288,24 @@
                 jnp.concatenate([source[first + u] for u in range(QUARTERS)], axis=1)
                 for source in (centre_ref, inverse_ref)
             )
-            for c in range(MAX_LEN // LANES):
+            if t - 2 in gates:
+                centre = centre + jnp.concatenate([gates[t - 2]] * QUARTERS, axis=1)
+            for c, span in enumerate(order):
                 rows = slice(c * LANES, (c + 1) * LANES)
                 values = jnp.concatenate(
-                    [base[first + u + c + 1] for u in range(QUARTERS)], axis=1
+                    [base[first + u + span + 1] for u in range(QUARTERS)], axis=1
                 )
-                normal = ((values - centre) * inverse).astype(jnp.bfloat16)
-                if k == 0:
-                    normal = normal * jnp.concatenate([keep_ref[rows, :]] * 2, axis=1)
+                scale = inverse
+                if k == 0 and c < parts_of - 1:
+                    scale = inverse * jnp.where(span < last, 1.0, 0.0)
+                normal = ((values - centre) * scale).astype(jnp.bfloat16)
+                if k == 0 and c == parts_of - 1:
+                    normal = normal * jnp.concatenate([keep_ref[...]] * 2, axis=1)
                 target[t, rows, :] = normal
 
     def product(t):
         row_block, col_block = blocks_of[t]
-        limit = excluded - (col_block - row_block) * TILE_SIDE
+        apart = jnp.minimum(col_block - row_block, 2) * (TILE_SIDE // SUBLANES)
         tops, found = [None] * QUARTERS, []
         for low in range(0, TILE_SIDE, 2 * LANES):
             values = lax.dot_general(
@@ -296,19 +314,28 @@
                 (((0,), (0,)), ((), ())),
                 preferred_element_type=jnp.float32,
             )
-            ahead = lax.broadcasted_iota(jnp.int32, values.shape, 1) - (
-                lax.broadcasted_iota(jnp.int32, values.shape, 0) + low
-            )
-            values = jnp.where(ahead > limit, values, -size)
+            bounds = [
+                jnp.concatenate(
+                    [
+                        bound_ref[apart + (TILE_SIDE + u * LANES - row) // SUBLANES - 1]
+                        for row in range(low, low + 2 * LANES, SUBLANES)
+                    ],
+                    axis=0,
+                )
+                for u in range(QUARTERS)
+            ]
             folded = None
             for u in range(QUARTERS):
-                part = values[:, u * LANES : (u + 1) * LANES]
+                part = jnp.minimum(values[:, u * LANES : (u + 1) * LANES], bounds[u])
                 folded = part if folded is None else jnp.maximum(folded, part)
-                top = jnp.max(part, axis=0, keepdims=True)
+                top = jnp.max(part.reshape(-1, SUBLANES, LANES), axis=0)
                 tops[u] = top if tops[u] is None else jnp.maximum(tops[u], top)
             for q in range(2):
                 turned_back = jnp.transpose(folded[q * LANES : (q + 1) * LANES, :])
                 found.append(jnp.max(turned_back, axis=0, keepdims=True))
+        tops = [jnp.max(top, axis=0, keepdims=True) for top in tops]
+        met = functools.reduce(jnp.maximum, [*found, *tops])
+        gates[t] = jnp.maximum(met - 1e30, 0.0)
         both = jnp.broadcast_to(found[0], sub.shape)
         for u, row in enumerate([*found[1:], *tops]):
             both = jnp.where(sub == u + 1, row, both)
@@ -403,6 +430,7 @@
     per = chunk * piece // LANES
     chunk_rows = (per + SUBLANES - 1) // SUBLANES * SUBLANES
     planes = len_devices if len_devices <= 2 else 1
+    bounds = (4 * TILE_SIDE - LANES) // SUBLANES
     share = count_len
     assert n % share == 0 and share & (share - 1) == 0
     dma = pltpu.SemaphoreType.DMA
@@ -433,7 +461,8 @@
             pltpu.VMEM((columns + 1, LANES, LANES), jnp.float32),
             pltpu.VMEM(depth, jnp.float32),
             pltpu.VMEM(depth, jnp.float32),
-            pltpu.VMEM((MAX_LEN, 2 * LANES), jnp.bfloat16),
+            pltpu.VMEM((LANES, 2 * LANES), jnp.bfloat16),
+            pltpu.VMEM((bounds, SUBLANES, LANES), jnp.float32),
             pltpu.VMEM((share * tile_list.shape[0], MAX_LEN, TILE_SIDE), jnp.bfloat16),
             pltpu.VMEM((share * tile_list.shape[0], MAX_LEN, TILE_SIDE), jnp.bfloat16),
             pltpu.VMEM((n, SUBLANES, LANES), jnp.float32),

time: 25.4 us -> 25 us (0.984)
  Pallas kernels: 24.6 us -> 24.2 us
    pallas_call x1, Pallas kernels: 23.9 us -> 23.6 us  [shards(): pl.pallas_call(functools.partial(profile_kernel, piece, n, count_len, len...]
where the time goes in v5:
time: 25 us; the launch traced here: 24.8 us
  Pallas kernels  24.2 us (97%)
  between operations  0.64 us (3%)
    pallas_call x1, Pallas kernels, shards(): pl.pallas_call(functools.partial(profile_kernel, piece, n, count_len, len...  23.6 us
    pallas_call x1, Pallas kernels, shards(): pl.pallas_call(write_kernel, out_shape=(profile, profile), in_specs=[pl.B...  0.63 us

profile of v5, /device:TPU:0, one launch (start us, length us, event | category | flops | bytes accessed | tf_op | source)
XLA Modules:
  0.0 24.8 jit_solution(15864872950582617037)
XLA Ops:
  0.6 23.6 %profile.1.groups_ref = f32[2,2,8,128]{3,2,1,0:T(8,128)S(1)} custom-call(f32[576]{0:T(1024)} %series_ref.1, s32[2,4]{1,0:T(2,128)} %bitcast.1, s32[2]{0:T(128)} %length_hbm.1, s32[2]{0:T(128)} %barrier_hbm.1), custom_call_target="tpu_custom_call" | custom-call | tf_op jit(solution)/shard_map/profile/pallas_call | solution.py:438
  24.2 0.6 %write_profiles.1 = (f32[4,512]{1,0:T(4,128)}, f32[4,512]{1,0:T(4,128)}) custom-call(f32[2,2,8,128]{3,2,1,0:T(8,128)S(1)} %profile.1.groups_ref), custom_call_target="tpu_custom_call" | custom-call | tf_op jit(solution)/shard_map/write_profiles/pallas_call | solution.py:496

commit v6 on v5

--- a/solution.py
+++ b/solution.py
@@ -167,6 +167,7 @@
         load.start()
 
     slot_rows = staged.shape[0]
+    used_rows = max(-(-(t * piece % LANES + piece) // LANES) for t in range(n))
     flat[...] = jnp.zeros(flat.shape, jnp.float32)
     loads[0].wait()
     flat[:piece] = piece_ref[...]
@@ -179,8 +180,8 @@
     pl.semaphore_wait(barrier, n - 1 + len_devices - 1)
     for step in range(n - 1, 0, -1):
         copy_to(
-            staged,
-            slots.at[me],
+            staged.at[pl.ds(0, used_rows)],
+            slots.at[me, pl.ds(0, used_rows)],
             send_piece,
             recv_piece.at[step // chunk],
             tile=partner(me, step, n),
@@ -249,7 +250,7 @@
         q = partner(lax.div(me, chunk), k, chunks)
         coming = chunk if k else chunk - 1
         if coming:
-            await_all(slots.at[pl.ds(0, coming)], recv_piece.at[k], False)
+            await_all(slots.at[pl.ds(0, coming), pl.ds(0, used_rows)], recv_piece.at[k], False)
         chunk_rows[q] = jnp.zeros(chunk_rows.shape[1:], jnp.float32)
         for t in range(chunk):
             low, first = divmod(t * piece, LANES)
@@ -268,7 +269,7 @@
 
     for copy in passed:
         copy.wait()
-    await_all(slots.at[pl.ds(0, n - 1)], send_piece, True)
+    await_all(slots.at[pl.ds(0, n - 1), pl.ds(0, used_rows)], send_piece, True)
     for q in range(chunks):
         packed[q * per : (q + 1) * per, :] = chunk_rows[q, :per, :]
     columns = packed.shape[0]
@@ -289,7 +290,7 @@
                 for source in (centre_ref, inverse_ref)
             )
             if t - 2 in gates:
-                centre = centre + jnp.concatenate([gates[t - 2]] * QUARTERS, axis=1)
+                centre = centre + jnp.concatenate([gates[t - 2][k]] * QUARTERS, axis=1)
             for c, span in enumerate(order):
                 rows = slice(c * LANES, (c + 1) * LANES)
                 values = jnp.concatenate(
@@ -303,81 +304,105 @@
                     normal = normal * jnp.concatenate([keep_ref[...]] * 2, axis=1)
                 target[t, rows, :] = normal
 
-    def product(t):
+    half = TILE_SIDE // 2
+
+    def product(t, row, col, width):
         row_block, col_block = blocks_of[t]
         apart = jnp.minimum(col_block - row_block, 2) * (TILE_SIDE // SUBLANES)
-        tops, found = [None] * QUARTERS, []
-        for low in range(0, TILE_SIDE, 2 * LANES):
-            values = lax.dot_general(
-                left_op[t, :, low : low + 2 * LANES],
-                right_op[t],
-                (((0,), (0,)), ((), ())),
-                preferred_element_type=jnp.float32,
+        values = lax.dot_general(
+            left_op[t, :, row : row + half],
+            right_op[t, :, col : col + width],
+            (((0,), (0,)), ((), ())),
+            preferred_element_type=jnp.float32,
+        )
+        folded, tops = None, []
+        for u in range(0, width, LANES):
+            bounds = jnp.concatenate(
+                [
+                    bound_ref[apart + (TILE_SIDE + col + u - line) // SUBLANES - 1]
+                    for line in range(row, row + half, SUBLANES)
+                ],
+                axis=0,
             )
-            bounds = [
-                jnp.concatenate(
-                    [
-                        bound_ref[apart + (TILE_SIDE + u * LANES - row) // SUBLANES - 1]
-                        for row in range(low, low + 2 * LANES, SUBLANES)
-                    ],
-                    axis=0,
-                )
-                for u in range(QUARTERS)
-            ]
-            folded = None
-            for u in range(QUARTERS):
-                part = jnp.minimum(values[:, u * LANES : (u + 1) * LANES], bounds[u])
-                folded = part if folded is None else jnp.maximum(folded, part)
-                top = jnp.max(part.reshape(-1, SUBLANES, LANES), axis=0)
-                tops[u] = top if tops[u] is None else jnp.maximum(tops[u], top)
-            for q in range(2):
-                turned_back = jnp.transpose(folded[q * LANES : (q + 1) * LANES, :])
-                found.append(jnp.max(turned_back, axis=0, keepdims=True))
-        tops = [jnp.max(top, axis=0, keepdims=True) for top in tops]
-        met = functools.reduce(jnp.maximum, [*found, *tops])
-        gates[t] = jnp.maximum(met - 1e30, 0.0)
-        both = jnp.broadcast_to(found[0], sub.shape)
-        for u, row in enumerate([*found[1:], *tops]):
-            both = jnp.where(sub == u + 1, row, both)
+            part = jnp.minimum(values[:, u : u + LANES], bounds)
+            folded = part if folded is None else jnp.maximum(folded, part)
+            tops.append(jnp.max(part.reshape(-1, SUBLANES, LANES), axis=0))
+        found = [
+            jnp.max(jnp.transpose(folded[u : u + LANES, :]), axis=0, keepdims=True)
+            for u in range(0, half, LANES)
+        ]
+        return found, tops
+
+    def larger(some, others):
+        return [jnp.maximum(x, y) for x, y in zip(some, others)]
+
+    lines4 = lax.broadcasted_iota(jnp.int32, (QUARTERS, LANES), 0)
+
+    def update(r, t, right, left):
+        row_block, col_block = blocks_of[t]
+        left = [jnp.max(top, axis=0, keepdims=True) for top in left]
+        both = jnp.broadcast_to(right[0], lines4.shape)
+        for u, line in enumerate([*right[1:], *left]):
+            both = jnp.where(lines4 == u + 1, line, both)
         both = 1.0 - both / size
         owner = jnp.where(
-            sub < QUARTERS, jnp.full(sub.shape, row_block), jnp.full(sub.shape, col_block)
+            lines4 < len(right),
+            jnp.full(lines4.shape, row_block),
+            jnp.full(lines4.shape, col_block),
         )
         for b in range(n):
-            best[b] = jnp.minimum(best[b], jnp.where(owner == b, both, EMPTY_VALUE))
-
+            best[r, b] = jnp.minimum(best[r, b], jnp.where(owner == b, both, EMPTY_VALUE))
+        return jnp.maximum(functools.reduce(jnp.maximum, [*right, *left]) - 1e30, 0.0)
+
+    def send(r):
+        for step in sorted(range(1, planes * n), key=lambda s: (s % n, s), reverse=True):
+            copy_to(
+                best.at[r, partner(me, step % n, n)],
+                parts.at[r, my_plane * n + step % n],
+                send_sem.at[r],
+                recv_sem.at[r],
+                len=partner(my_len, step // n, len_devices),
+                tile=partner(me, step % n, n),
+            ).start()
+        parts[r, my_plane * n] = best[r, me]
+
+    kept = {}
     build(0)
     for t in range(len(tiles)):
         if t + 1 < len(tiles):
             build(t + 1)
-        product(t)
-
+        found, tops = product(t, 0, 0, TILE_SIDE)
+        found_below, tops_below = product(t, half, 0, half)
+        gates[t] = (
+            jnp.maximum(found[0] - 1e30, 0.0),
+            update(0, t, found, larger(tops[:2], tops_below)),
+        )
+        kept[t] = found_below, tops[2:]
     if planes > 1:
         pl.semaphore_wait(plane_sem, len_devices - 1)
-    for step in sorted(range(1, planes * n), key=lambda s: (s % n, s), reverse=True):
-        copy_to(
-            best.at[partner(me, step % n, n)],
-            parts.at[my_plane * n + step % n],
-            send_sem,
-            recv_sem,
-            len=partner(my_len, step // n, len_devices),
-            tile=partner(me, step % n, n),
-        ).start()
-    parts[my_plane * n] = best[me]
-    everyone = parts.at[pl.ds(0, planes * n - 1)]
-    await_all(everyone, send_sem, True)
-    await_all(everyone, recv_sem, False)
-    for g in range(planes):
-        for e in range(share):
-            merged = parts[g * n + e]
-            for step in range(e + share, n, share):
-                merged = jnp.minimum(merged, parts[g * n + step])
-            l = partner(turn_of_mine, e, share)
-            if planes > 1:
-                groups[g, l] = merged
-            else:
-                mine[l] = merged
-                groups[my_len, l] = merged
+    send(0)
+    for t in range(len(tiles)):
+        found, tops = product(t, half, half, half)
+        found_before, tops_before = kept[t]
+        update(1, t, larger(found, found_before), larger(tops, tops_before))
+    send(1)
+
+    everyone = parts.at[0, pl.ds(0, planes * n - 1)]
+    for r in range(2):
+        await_all(everyone, send_sem.at[r], True)
+    for r in range(2):
+        await_all(everyone, recv_sem.at[r], False)
+        for g in range(planes):
+            for e in range(share):
+                merged = parts[r, g * n + e]
+                for step in range(e + share, n, share):
+                    merged = jnp.minimum(merged, parts[r, g * n + step])
+                l = partner(turn_of_mine, e, share)
+                if planes > 1:
+                    groups[g, l, r] = merged
+                else:
+                    mine[l, r] = merged
+                    groups[my_len, l, r] = merged
     if planes == 1:
         hops = [
             copy_to(
@@ -402,8 +427,9 @@
             row = g * count_len + l
             for u in range(QUARTERS):
                 lanes = slice(u * LANES, (u + 1) * LANES)
-                right[row : row + 1, lanes] = groups_ref[g, l, u : u + 1, :]
-                left[row : row + 1, lanes] = groups_ref[g, l, QUARTERS + u : QUARTERS + u + 1, :]
+                line = u % 2
+                right[row : row + 1, lanes] = groups_ref[g, l, u // 2, line : line + 1, :]
+                left[row : row + 1, lanes] = groups_ref[g, l, u // 2, line + 2 : line + 3, :]
     copies = [
         pltpu.make_async_copy(right, right_ref, sems.at[0]),
         pltpu.make_async_copy(left, left_ref, sems.at[1]),
@@ -445,7 +471,7 @@
             planes,
             chunk,
         ),
-        out_shape=pltpu.VMEM((len_devices, count_len, SUBLANES, LANES), jnp.float32),
+        out_shape=pltpu.VMEM((len_devices, count_len, 2, QUARTERS, LANES), jnp.float32),
         in_specs=[pl.BlockSpec(memory_space=HBM)] * 4,
         out_specs=pl.BlockSpec(memory_space=VMEM),
         scratch_shapes=[
@@ -465,17 +491,17 @@
             pltpu.VMEM((bounds, SUBLANES, LANES), jnp.float32),
             pltpu.VMEM((share * tile_list.shape[0], MAX_LEN, TILE_SIDE), jnp.bfloat16),
             pltpu.VMEM((share * tile_list.shape[0], MAX_LEN, TILE_SIDE), jnp.bfloat16),
-            pltpu.VMEM((n, SUBLANES, LANES), jnp.float32),
-            pltpu.VMEM((planes * n, SUBLANES, LANES), jnp.float32),
-            pltpu.VMEM((count_len, SUBLANES, LANES), jnp.float32),
+            pltpu.VMEM((2, n, QUARTERS, LANES), jnp.float32),
+            pltpu.VMEM((2, planes * n, QUARTERS, LANES), jnp.float32),
+            pltpu.VMEM((count_len, 2, QUARTERS, LANES), jnp.float32),
             dma((4,)),
             dma((share,)),
             dma((share,)),
             pltpu.SemaphoreType.REGULAR,
             dma,
             dma((n // chunk,)),
-            dma,
-            dma,
+            dma((2,)),
+            dma((2,)),
             dma((len_devices,)),
             dma((len_devices,)),
         ],

time: 25 us -> 24.6 us (0.984)
  Pallas kernels: 24.2 us -> 23.8 us
    pallas_call x1, Pallas kernels: 23.6 us -> 23.1 us  [shards(): pl.pallas_call(functools.partial(profile_kernel, piece, n, count_len, len...]
where the time goes in v6:
time: 24.6 us; the launch traced here: 24.4 us
  Pallas kernels  23.8 us (97%)
  between operations  0.64 us (3%)
    pallas_call x1, Pallas kernels, shards(): pl.pallas_call(functools.partial(profile_kernel, piece, n, count_len, len...  23.1 us
    pallas_call x1, Pallas kernels, shards(): pl.pallas_call(write_kernel, out_shape=(profile, profile), in_specs=[pl.B...  0.63 us

profile of v6, /device:TPU:0, one launch (start us, length us, event | category | flops | bytes accessed | tf_op | source)
XLA Modules:
  0.0 24.4 jit_solution(5003928959084134806)
XLA Ops:
  0.6 23.1 %profile.1.groups_ref = f32[2,2,2,4,128]{4,3,2,1,0:T(4,128)S(1)} custom-call(f32[576]{0:T(1024)} %series_ref.1, s32[2,4]{1,0:T(2,128)} %bitcast.1, s32[2]{0:T(128)} %length_hbm.1, s32[2]{0:T(128)} %barrier_hbm.1), custom_call_target="tpu_custom_call" | custom-call | tf_op jit(solution)/shard_map/profile/pallas_call | solution.py:464
  23.8 0.6 %write_profiles.1 = (f32[4,512]{1,0:T(4,128)}, f32[4,512]{1,0:T(4,128)}) custom-call(f32[2,2,2,4,128]{4,3,2,1,0:T(4,128)S(1)} %profile.1.groups_ref), custom_call_target="tpu_custom_call" | custom-call | tf_op jit(solution)/shard_map/write_profiles/pallas_call | solution.py:522

commit v7 on v6

--- a/solution.py
+++ b/solution.py
@@ -389,8 +389,6 @@
 
     everyone = parts.at[0, pl.ds(0, planes * n - 1)]
     for r in range(2):
-        await_all(everyone, send_sem.at[r], True)
-    for r in range(2):
         await_all(everyone, recv_sem.at[r], False)
         for g in range(planes):
             for e in range(share):
@@ -403,6 +401,8 @@
                 else:
                     mine[l, r] = merged
                     groups[my_len, l, r] = merged
+    for r in range(2):
+        await_all(everyone, send_sem.at[r], True)
     if planes == 1:
         hops = [
             copy_to(

time: 24.6 us -> 24.6 us (level)
  no operation moved by 1% of the time
where the time goes in v7:
time: 24.6 us; the launch traced here: 24.4 us
  Pallas kernels  23.8 us (97%)
  between operations  0.64 us (3%)
    pallas_call x1, Pallas kernels, shards(): pl.pallas_call(functools.partial(profile_kernel, piece, n, count_len, len...  23.1 us
    pallas_call x1, Pallas kernels, shards(): pl.pallas_call(write_kernel, out_shape=(profile, profile), in_specs=[pl.B...  0.63 us

profile of v7, /device:TPU:0, one launch (start us, length us, event | category | flops | bytes accessed | tf_op | source)
XLA Modules:
  0.0 24.4 jit_solution(14900755429078376544)
XLA Ops:
  0.6 23.1 %profile.1.groups_ref = f32[2,2,2,4,128]{4,3,2,1,0:T(4,128)S(1)} custom-call(f32[576]{0:T(1024)} %series_ref.1, s32[2,4]{1,0:T(2,128)} %bitcast.1, s32[2]{0:T(128)} %length_hbm.1, s32[2]{0:T(128)} %barrier_hbm.1), custom_call_target="tpu_custom_call" | custom-call | tf_op jit(solution)/shard_map/profile/pallas_call | solution.py:464
  23.8 0.6 %write_profiles.1 = (f32[4,512]{1,0:T(4,128)}, f32[4,512]{1,0:T(4,128)}) custom-call(f32[2,2,2,4,128]{4,3,2,1,0:T(4,128)S(1)} %profile.1.groups_ref), custom_call_target="tpu_custom_call" | custom-call | tf_op jit(solution)/shard_map/write_profiles/pallas_call | solution.py:522
